TPU v7x, 32 devices: a whole 2x2x4 slice. The times are simulated.
32 devices in a mesh: groups: 2 (over y), chan: 8 (over z, x), sub: 2 (over core).
Axes of the slice: x: 2, y: 2, z: 4, core: 2. Of those that a mesh axis runs over, the one named last changes fastest.
Arguments:
- predicted_sky_response: bfloat16 [16384, 8, 2, 128], P(('groups', 'chan', 'sub')), parts along dimension 0, may hold values from -0.4375 to 0.4375
- measured_correlation: bfloat16 [16384, 2, 128], P(('groups', 'chan', 'sub')), parts along dimension 0, may hold values from -6 to 6
- keep_indicator: int32 [16384, 128], P(('groups', 'chan', 'sub')), parts along dimension 0, may hold values 0 or 1
- tile_owner: int32 [16384, 1], P(('groups', 'chan', 'sub')), parts along dimension 0, may hold values from 0 to 7; in each aligned block of 512 rows (0 to 511, 512 to 1023, ...) at most 192 rows name the same one
- tile_channel: int32 [16384], P(('groups', 'chan', 'sub')), parts along dimension 0, may hold values from 0 to 3
- tile_base: int32 [16384], P(('groups', 'chan', 'sub')), parts along dimension 0, may hold values from 0 to 14
- pairs: int32 [15, 2, 128], replicated, may hold values from 0 to 61, as said below
- gains: float32 [64, 2, 62, 8], P(('groups', 'chan')), parts along dimension 0, may hold values from -5 to 5
- duals: float32 [64, 2, 62, 8], P(('groups', 'chan', 'sub')), parts along dimension 0, may hold values from -4 to 4
- consensus: float32 [8, 2, 62, 8], P('groups'), parts along dimension 0, may hold values from -5 to 5
- rho: float32 [8], replicated, may hold values from 0.3 to 3
Outputs:
- gains_new: float32 [64, 2, 62, 8], P(('groups', 'chan', 'sub')), parts along dimension 0
- consensus_new: float32 [8, 2, 62, 8], P('groups'), parts along dimension 0
- duals_new: float32 [64, 2, 62, 8], P(('groups', 'chan', 'sub')), parts along dimension 0
There are 2 independent parts, one for each index of `groups`. A program takes and returns all parts, laid end to end along the dimension named above; an argument that names none is the same for every part. Nothing has to cross between parts.
Inputs may be any that keep to these rules, and one draw needn't show every extreme that they name: `tile_owner`: on the tiles of one device at most 192 name the same owner, a bound that some block reaches. `pairs`: the two stations of a row differ.
All inputs are finite; a program needn't handle non-finite values. No bound on the sum of `keep_indicator` on one device may be relied on, other than what follows from the above.
Results may differ from a plain program's by a relative error of at most 0.0027.
Values may be sent and summed in bfloat16 or wider, within the bound.
A program may use at most 128 MiB of HBM per device.

v0:
```python
import functools
import math

import jax
import jax.numpy as jnp
import numpy as np
from jax import lax
from jax.experimental import pallas as pl
from jax.experimental.pallas import tpu as pltpu
from jax.sharding import PartitionSpec as P

LANES = 128


def hermitian_rows(real, imag, upper):
    half = real.shape[0] // 2
    groups_real = [real * real + imag * imag]
    groups_imag = []
    for shift in range(1, half + 1):
        turned_real = pltpu.roll(real, 2 * half - shift, axis=0)
        turned_imag = pltpu.roll(imag, 2 * half - shift, axis=0)
        groups_real.append(real * turned_real + imag * turned_imag)
        groups_imag.append(real * turned_imag - imag * turned_real)
    mixed = jnp.where(upper, groups_real.pop(), groups_imag.pop())
    return groups_real + groups_imag + [mixed]


def accumulate_kernel(
    block,
    unroll,
    half,
    sub_count,
    owner_ref,
    channel_ref,
    base_ref,
    coupling_ref,
    observed_ref,
    keep_ref,
    pairs_ref,
    gains_ref,
    out_ref,
    table,
    turned,
    coupling_f,
    observed_f,
    keep_f,
):
    step = pl.program_id(0)
    bases = pairs_ref.shape[0]
    tile_rows = keep_ref.shape[1]
    width = LANES // half
    directions = gains_ref.shape[1]

    @pl.when(step == 0)
    def _():
        out_ref[...] = jnp.zeros_like(out_ref)
        turned[...] = jnp.zeros_like(turned)
        for base in range(bases):
            turned[2 * base : 2 * base + 2, :] = pairs_ref[base].astype(jnp.float32)
        columns = jnp.transpose(turned[...])
        lane = lax.broadcasted_iota(jnp.int32, (tile_rows, LANES), 1).astype(jnp.float32)
        for base in range(bases):
            for end in range(2):
                station = jnp.broadcast_to(
                    columns[:, 2 * base + end : 2 * base + end + 1], lane.shape
                )
                for part in range(half):
                    table[base * half + part, end * tile_rows : (end + 1) * tile_rows, :] = (
                        jnp.where(station == lane - float(part * width), 1.0, 0.0).astype(jnp.bfloat16)
                    )

    coupling_f[...] = coupling_ref[...].astype(jnp.float32)
    observed_f[...] = observed_ref[...].astype(jnp.float32)
    keep_f[...] = jnp.where(keep_ref[...] > 0, 1.0, 0.0)
    upper = lax.broadcasted_iota(jnp.int32, (directions, LANES), 0) < directions // 2

    def spread(row):
        return jnp.broadcast_to(row, (directions, LANES))

    def one_tile(local):
        tile = step * block + local
        channel = channel_ref[tile]
        base = base_ref[tile]
        owner = owner_ref[tile] * sub_count + lax.div(channel, half)
        place = lax.rem(channel, half)
        kept = spread(keep_f[pl.ds(local, 1), :])
        first = local * 2 * directions
        real = coupling_f[pl.ds(first, directions, stride=2), :] * kept
        imag = coupling_f[pl.ds(first + 1, directions, stride=2), :] * kept
        seen_real = spread(observed_f[pl.ds(2 * local, 1), :])
        seen_imag = spread(observed_f[pl.ds(2 * local + 1, 1), :])
        near = spread(pairs_ref[base, pl.ds(0, 1), :])
        far = spread(pairs_ref[base, pl.ds(1, 1), :])
        near, far = near + place * width, far + place * width
        gain_real = gains_ref[2 * owner]
        gain_imag = gains_ref[2 * owner + 1]

        def pick(values, index):
            return jnp.take_along_axis(values, index, axis=1, mode="promise_in_bounds")

        near_real, near_imag = pick(gain_real, near), pick(gain_imag, near)
        far_real, far_imag = pick(gain_real, far), pick(gain_imag, far)
        slope_real = real * far_real + imag * far_imag
        slope_imag = imag * far_real - real * far_imag
        mirror_real = real * near_real - imag * near_imag
        mirror_imag = -(real * near_imag + imag * near_real)

        def end_rows(vector_real, vector_imag, weight_real, weight_imag):
            side_real = vector_real * weight_real + vector_imag * weight_imag
            side_imag = vector_real * weight_imag - vector_imag * weight_real
            groups = hermitian_rows(vector_real, vector_imag, upper)
            whole = jnp.concatenate(groups, axis=0).astype(jnp.bfloat16)
            side = jnp.concatenate([side_real, side_imag], axis=0)
            high = side.astype(jnp.bfloat16)
            low = (side - high.astype(jnp.float32)).astype(jnp.bfloat16)
            return jnp.concatenate([whole, high, low], axis=0)

        rows = jnp.concatenate(
            [
                end_rows(slope_real, slope_imag, seen_real, seen_imag),
                end_rows(mirror_real, mirror_imag, seen_real, -seen_imag),
            ],
            axis=1,
        )
        sums = jnp.dot(rows, table[base * half + place], preferred_element_type=jnp.float32)
        normal_rows = directions * directions
        return owner, jnp.concatenate(
            [
                sums[:normal_rows],
                sums[normal_rows : normal_rows + 2 * directions] + sums[normal_rows + 2 * directions :],
            ],
            axis=0,
        )

    def one_group(group, carry):
        results = [one_tile(group * unroll + number) for number in range(unroll)]
        for owner, sums in results:
            out_ref[owner] += sums
        return carry

    lax.fori_loop(0, block // unroll, one_group, 0)


def accumulate(coupling, observed, keep, owner, channel, base, pairs, gain_table, half, sub_count):
    tiles, directions, _, tile_rows = coupling.shape
    owners = gain_table.shape[0] // 2
    bases = pairs.shape[0]
    block = min(64, tiles)
    unroll = math.gcd(block, 64)
    kernel = functools.partial(accumulate_kernel, block, unroll, half, sub_count)
    out_rows = directions * directions + 2 * directions
    return pl.pallas_call(
        kernel,
        grid_spec=pltpu.PrefetchScalarGridSpec(
            num_scalar_prefetch=3,
            grid=(tiles // block,),
            in_specs=[
                pl.BlockSpec((block * 2 * directions, tile_rows), lambda i, *_: (i, 0)),
                pl.BlockSpec((block * 2, tile_rows), lambda i, *_: (i, 0)),
                pl.BlockSpec((block, tile_rows), lambda i, *_: (i, 0)),
                pl.BlockSpec(pairs.shape, lambda i, *_: (0, 0, 0)),
                pl.BlockSpec(gain_table.shape, lambda i, *_: (0, 0, 0)),
            ],
            out_specs=pl.BlockSpec(
                (owners, out_rows, LANES), lambda i, *_: (0, 0, 0)
            ),
            scratch_shapes=[
                pltpu.VMEM((bases * half, 2 * tile_rows, LANES), jnp.bfloat16),
                pltpu.VMEM((LANES, tile_rows), jnp.float32),
                pltpu.VMEM((block * 2 * directions, tile_rows), jnp.float32),
                pltpu.VMEM((block * 2, tile_rows), jnp.float32),
                pltpu.VMEM((block, tile_rows), jnp.float32),
            ],
        ),
        out_shape=jax.ShapeDtypeStruct((owners, out_rows, LANES), jnp.float32),
        compiler_params=pltpu.CompilerParams(
            dimension_semantics=("arbitrary",), vmem_limit_bytes=60 << 20
        ),
    )(
        owner,
        channel,
        base,
        coupling.reshape(tiles * 2 * directions, tile_rows),
        observed.reshape(tiles * 2, tile_rows),
        keep,
        pairs,
        gain_table,
    )


def lay_pair(load, pad, half, width):
    total = None
    for part in range(half):
        block = load(part)
        pad[part % 2, :, : block.shape[1]] = block
        value = pad[part % 2]
        if part:
            value = pltpu.roll(value, part * width, axis=1)
        total = value if total is None else total + value
    return total


def gather_kernel(chan_count, sub_count, half, gains_ref, out_ref, pad, send_sem, recv_sem):
    chan = lax.axis_index("chan")
    width = LANES // half
    pad[...] = jnp.zeros_like(pad)
    for owner in range(sub_count):
        for part in range(2):
            out_ref[chan, owner, part] = lay_pair(
                lambda number: gains_ref[owner * half + number, part], pad, half, width
            )
    barrier = pltpu.get_barrier_semaphore()
    for offset in range(1, chan_count):
        pl.semaphore_signal(
            barrier,
            inc=1,
            device_id={"chan": lax.rem(chan + offset, chan_count)},
            device_id_type=pl.DeviceIdType.MESH,
        )
    pl.semaphore_wait(barrier, chan_count - 1)
    copies = []
    for offset in range(1, chan_count):
        copy = pltpu.make_async_remote_copy(
            src_ref=out_ref.at[chan],
            dst_ref=out_ref.at[chan],
            send_sem=send_sem.at[offset],
            recv_sem=recv_sem.at[offset],
            device_id={"chan": lax.rem(chan + offset, chan_count)},
            device_id_type=pl.DeviceIdType.MESH,
        )
        copy.start()
        copies.append(copy)
    for copy in copies:
        copy.wait()


def gather_gains(gains, chan_count, sub_count):
    channels_here, _, directions, _ = gains.shape
    half = channels_here // sub_count
    return pl.pallas_call(
        functools.partial(gather_kernel, chan_count, sub_count, half),
        out_shape=jax.ShapeDtypeStruct(
            (chan_count, sub_count, 2, directions, LANES), jnp.float32
        ),
        in_specs=[pl.BlockSpec(memory_space=pltpu.VMEM)],
        out_specs=pl.BlockSpec(memory_space=pltpu.VMEM),
        scratch_shapes=[
            pltpu.VMEM((2, directions, LANES), jnp.float32),
            pltpu.SemaphoreType.DMA((chan_count,)),
            pltpu.SemaphoreType.DMA((chan_count,)),
        ],
        compiler_params=pltpu.CompilerParams(collective_id=1, has_side_effects=True),
    )(gains)


def solve_hermitian(groups_real, groups_imag, mixed, ridge, side_real, side_imag):
    directions = side_real.shape[0]
    middle = directions // 2
    row = lax.broadcasted_iota(jnp.int32, side_real.shape, 0)
    upper = row < middle
    swapped = pltpu.roll(mixed, middle, axis=0)
    real = {0: groups_real[0] + ridge, middle: jnp.where(upper, mixed, swapped)}
    imag = {0: jnp.zeros_like(ridge), middle: jnp.where(upper, -swapped, mixed)}
    for d in range(1, middle):
        real[d], imag[d] = groups_real[d], groups_imag[d - 1]
        real[directions - d] = pltpu.roll(groups_real[d], d, axis=0)
        imag[directions - d] = -pltpu.roll(groups_imag[d - 1], d, axis=0)
    columns = []
    for l in range(directions):
        column_real, column_imag = real[l], imag[l]
        for k in range(1, directions):
            here = row == k
            d = (l - k) % directions
            column_real = jnp.where(here, real[d], column_real)
            column_imag = jnp.where(here, imag[d], column_imag)
        columns.append((column_real, column_imag))
    columns.append((side_real, side_imag))
    scale = jnp.zeros_like(ridge)
    for j in range(directions):
        pivot_real, pivot_imag = columns[j]
        inverse = 1.0 / pivot_real[j : j + 1]
        here = row == j
        scale = jnp.where(here, jnp.broadcast_to(inverse, scale.shape), scale)
        factor_real = jnp.where(here, 0.0, pivot_real * inverse)
        factor_imag = jnp.where(here, 0.0, pivot_imag * inverse)
        for l in range(j + 1, directions + 1):
            value_real, value_imag = columns[l]
            head_real, head_imag = value_real[j : j + 1], value_imag[j : j + 1]
            columns[l] = (
                value_real - (factor_real * head_real - factor_imag * head_imag),
                value_imag - (factor_real * head_imag + factor_imag * head_real),
            )
    return columns[-1][0] * scale, columns[-1][1] * scale


def basis_of(channel, channels):
    x = (2.0 * channel - (channels - 1)) / max(channels - 1, 1)
    return [
        jnp.ones_like(x),
        x,
        0.5 * (3.0 * x * x - 1.0),
        0.5 * (5.0 * x * x * x - 3.0 * x),
    ]


def inverse_gram(channels):
    f = np.arange(channels, dtype=np.float64)
    x = (2.0 * f - (channels - 1)) / max(channels - 1, 1)
    basis = np.stack([np.ones_like(x), x, 0.5 * (3 * x * x - 1), 0.5 * (5 * x * x * x - 3 * x)])
    return np.linalg.inv(basis @ basis.T)


def encode(sums, directions):
    normal_rows = directions * directions
    side = sums[normal_rows:]
    high = side.astype(jnp.bfloat16)
    low = (side - high.astype(jnp.float32)).astype(jnp.bfloat16)
    return jnp.concatenate([sums[:normal_rows].astype(jnp.bfloat16), high, low], axis=0)


def decode(coded, directions):
    wide = coded.astype(jnp.float32)
    normal_rows = directions * directions
    side_rows = 2 * directions
    high, low = wide[normal_rows : normal_rows + side_rows], wide[normal_rows + side_rows :]
    return jnp.concatenate([wide[:normal_rows], high + low], axis=0)


def finish_kernel(
    chan_count,
    sub_count,
    half,
    rho_ref,
    packed_ref,
    duals_ref,
    consensus_ref,
    gains_out,
    consensus_out,
    duals_out,
    pad,
    near_src,
    near_buf,
    send_buf,
    far_buf,
    weights,
    basis_buf,
    near_send,
    near_recv,
    far_send,
    far_recv,
    last_send,
    last_recv,
):
    chan, sub = lax.axis_index("chan"), lax.axis_index("sub")
    owners = chan_count * sub_count
    channels = owners * half
    width = LANES // half
    directions, stations = duals_ref.shape[2], duals_ref.shape[3]
    degree = consensus_ref.shape[0]
    me = chan * sub_count + sub

    def device(flat):
        return {"chan": lax.div(flat, sub_count), "sub": lax.rem(flat, sub_count)}

    barrier = pltpu.get_barrier_semaphore()
    for offset in range(1, owners):
        pl.semaphore_signal(
            barrier,
            inc=1,
            device_id=device(lax.rem(me + offset, owners)),
            device_id_type=pl.DeviceIdType.MESH,
        )
    order = list(range(1, chan_count)) + [0]
    for offset in order:
        target = lax.rem(chan + offset, chan_count)
        for shift in range(1, sub_count):
            near_src[shift - 1, offset] = encode(
                packed_ref[target, lax.rem(sub + shift, sub_count)], directions
            )
    pl.semaphore_wait(barrier, owners - 1)

    near = {}
    for offset in order:
        for shift in range(1, sub_count):
            other = lax.rem(sub + shift, sub_count)
            copy = pltpu.make_async_remote_copy(
                src_ref=near_src.at[shift - 1, offset],
                dst_ref=near_buf.at[shift - 1, offset],
                send_sem=near_send.at[shift - 1, offset],
                recv_sem=near_recv.at[shift - 1, offset],
                device_id={"sub": other},
                device_id_type=pl.DeviceIdType.MESH,
            )
            copy.start()
            near[offset, shift] = copy

    pad[...] = jnp.zeros_like(pad)
    shape = (directions, LANES)
    row = lax.broadcasted_iota(jnp.int32, shape, 0)
    rho = jnp.zeros(shape, jnp.float32)
    for k in range(directions):
        rho = jnp.where(row == k, rho_ref[k], rho)
    lane = lax.broadcasted_iota(jnp.int32, (owners, LANES), 1)
    owner = lax.broadcasted_iota(jnp.int32, (owners, LANES), 0)
    everyone = basis_of((owner * half + lax.div(lane, width)).astype(jnp.float32), channels)
    for d in range(degree):
        basis_buf[d] = everyone[d]
    mine = [jnp.broadcast_to(basis_buf[d, pl.ds(me, 1), :], shape) for d in range(degree)]
    duals = [
        lay_pair(lambda number: duals_ref[number, part], pad, half, width) for part in range(2)
    ]
    anchors = []
    for part in range(2):
        anchor = jnp.zeros(shape, jnp.float32)
        for d in range(degree):
            anchor = anchor + mine[d] * lay_pair(
                lambda number: consensus_ref[d, part], pad, half, width
            )
        anchors.append(anchor)

    far = []
    for offset in order:
        target = lax.rem(chan + offset, chan_count)
        total = packed_ref[target, sub]
        for shift in range(1, sub_count):
            near[offset, shift].wait_recv()
            total = total + decode(near_buf[shift - 1, offset], directions)
        if offset:
            send_buf[offset] = encode(total, directions)
            copy = pltpu.make_async_remote_copy(
                src_ref=send_buf.at[offset],
                dst_ref=far_buf.at[offset],
                send_sem=far_send.at[offset],
                recv_sem=far_recv.at[offset],
                device_id={"chan": target},
                device_id_type=pl.DeviceIdType.MESH,
            )
            copy.start()
            far.append((offset, copy))
    for offset, copy in far:
        copy.wait_recv()
        total = total + decode(far_buf[offset], directions)

    middle = directions // 2
    group = [total[i * directions : (i + 1) * directions] for i in range(directions + 2)]
    solved = solve_hermitian(
        group[:middle],
        group[middle : directions - 1],
        group[directions - 1],
        rho,
        group[directions] - duals[0] + rho * anchors[0],
        group[directions + 1] - duals[1] + rho * anchors[1],
    )
    for part in range(2):
        weights[me, part] = solved[part] + duals[part] / rho

    last = []
    for offset in range(1, owners):
        copy = pltpu.make_async_remote_copy(
            src_ref=weights.at[me],
            dst_ref=weights.at[me],
            send_sem=last_send.at[offset],
            recv_sem=last_recv.at[offset],
            device_id=device(lax.rem(me + offset, owners)),
            device_id_type=pl.DeviceIdType.MESH,
        )
        copy.start()
        last.append(copy)

    def store(ref, part, value):
        for number in range(half):
            turned = pltpu.roll(value, LANES - number * width, axis=1) if number else value
            ref[number, part] = turned[:, :stations]

    for part in range(2):
        store(gains_out, part, solved[part])
    for copy in last:
        copy.wait_recv()
    inverse = inverse_gram(channels)
    for part in range(2):
        totals = []
        for d in range(degree):
            value = jnp.zeros(shape, jnp.float32)
            for number in range(owners):
                value = value + basis_buf[d, number : number + 1, :] * weights[number, part]
            folded = value
            for number in range(1, half):
                folded = folded + pltpu.roll(value, number * width, axis=1)
            totals.append(folded)
        fitted = jnp.zeros(shape, jnp.float32)
        for d in range(degree):
            value = sum(float(inverse[d, e]) * totals[e] for e in range(degree))
            consensus_out[d, part] = value[:, :stations]
            fitted = fitted + mine[d] * value
        store(duals_out, part, duals[part] + rho * (solved[part] - fitted))
    for copy in near.values():
        copy.wait_send()
    for _, copy in far:
        copy.wait_send()
    for copy in last:
        copy.wait_send()


def finish(rho, packed, duals, consensus, chan_count, sub_count):
    half, _, directions, stations = duals.shape
    _, _, rows, _ = packed.shape
    owners = chan_count * sub_count
    degree = consensus.shape[0]
    coded = rows + 2 * directions
    vmem = pl.BlockSpec(memory_space=pltpu.VMEM)
    dma = pltpu.SemaphoreType.DMA
    return pl.pallas_call(
        functools.partial(finish_kernel, chan_count, sub_count, half),
        out_shape=(
            jax.ShapeDtypeStruct(duals.shape, jnp.float32),
            jax.ShapeDtypeStruct(consensus.shape, jnp.float32),
            jax.ShapeDtypeStruct(duals.shape, jnp.float32),
        ),
        in_specs=[pl.BlockSpec(memory_space=pltpu.SMEM), vmem, vmem, vmem],
        out_specs=(vmem, vmem, vmem),
        scratch_shapes=[
            pltpu.VMEM((2, directions, LANES), jnp.float32),
            pltpu.VMEM((sub_count - 1, chan_count, coded, LANES), jnp.bfloat16),
            pltpu.VMEM((sub_count - 1, chan_count, coded, LANES), jnp.bfloat16),
            pltpu.VMEM((chan_count, coded, LANES), jnp.bfloat16),
            pltpu.VMEM((chan_count, coded, LANES), jnp.bfloat16),
            pltpu.VMEM((owners, 2, directions, LANES), jnp.float32),
            pltpu.VMEM((degree, owners, LANES), jnp.float32),
            dma((sub_count - 1, chan_count)),
            dma((sub_count - 1, chan_count)),
            dma((chan_count,)),
            dma((chan_count,)),
            dma((owners,)),
            dma((owners,)),
        ],
        compiler_params=pltpu.CompilerParams(
            collective_id=2, has_side_effects=True, vmem_limit_bytes=60 << 20
        ),
    )(rho, packed, duals, consensus)


def body(
    predicted_sky_response,
    measured_correlation,
    keep_indicator,
    tile_owner,
    tile_channel,
    tile_base,
    pairs,
    gains,
    duals,
    consensus,
    rho,
):
    channels_here, _, _, directions = gains.shape
    chan_count = lax.axis_size("chan")
    sub_count = lax.axis_size("sub")
    half = channels_here // sub_count
    all_gains = gather_gains(jnp.swapaxes(gains, 2, 3), chan_count, sub_count)
    packed = accumulate(
        predicted_sky_response,
        measured_correlation,
        keep_indicator,
        tile_owner[:, 0],
        tile_channel,
        tile_base,
        pairs,
        all_gains.reshape(-1, directions, LANES),
        half,
        sub_count,
    )
    outputs = finish(
        rho,
        packed.reshape((chan_count, sub_count) + packed.shape[1:]),
        jnp.swapaxes(duals, 2, 3),
        jnp.swapaxes(consensus, 2, 3),
        chan_count,
        sub_count,
    )
    return tuple(jnp.swapaxes(x, 2, 3) for x in outputs)


def solution(mesh):
    placed = (
        P(("groups", "chan", "sub"), None, None, None),
        P(("groups", "chan", "sub"), None, None),
        P(("groups", "chan", "sub"), None),
        P(("groups", "chan", "sub"), None),
        P(("groups", "chan", "sub")),
        P(("groups", "chan", "sub")),
        P(),
        P(("groups", "chan"), None, None, None),
        P(("groups", "chan", "sub"), None, None, None),
        P("groups", None, None, None),
        P(),
    )
    return jax.shard_map(
        body,
        mesh=mesh,
        in_specs=placed,
        out_specs=(
            P(("groups", "chan", "sub"), None, None, None),
            P("groups", None, None, None),
            P(("groups", "chan", "sub"), None, None, None),
        ),
        check_vma=False,
    )
```

profile of v0, /device:TPU:0, one launch (start us, length us, event | category | flops | bytes accessed | tf_op | source)
XLA Modules:
  0.0 52.3 jit_solution(6191325881042279324)
XLA Ops:
  0.6 10.8 %shard_map.130 = f32[8,2,2,8,128]{4,3,2,1,0:T(8,128)} custom-call(f32[4,2,8,62]{3,2,1,0:T(8,128)} %bitcast.15), custom_call_target="tpu_custom_call" | custom-call | tf_op jit(solution)/shard_map/pallas_call | solution.py:240
  11.5 17.9 %shard_map.131 = f32[16,80,128]{2,1,0:T(8,128)} custom-call(s32[512]{0:T(512)} %bitcast.21, s32[512]{0:T(512)} %channel_ref.1, s32[512]{0:T(512)} %base_ref.1, bf16[8192,128]{1,0:T(8,128)(2,1)} %bitcast.12, bf16[1024,128]{1,0:T(8,128)(2,1)} %bitcast.14, s32[512,128]{1,0:T(8,128)} %keep_ref.1, s32[15,2,128]{2,1,0:T(2,128)} %pairs_ref.1, f32[32,8,128]{2,1,0:T(8,128)} %bitcast.13), custom_call_target="tpu_custom_call" | custom-call | tf_op jit(solution)/shard_map/pallas_call | solution.py:152
  29.4 18.9 %shard_map.132 = (f32[2,2,8,62]{3,2,1,0:T(8,128)}, f32[4,2,8,62]{3,2,1,0:T(8,128)}, f32[2,2,8,62]{3,2,1,0:T(8,128)}) custom-call(f32[8]{0:T(128)} %rho_ref.1, f32[8,2,80,128]{3,2,1,0:T(8,128)} %bitcast.11, f32[2,2,8,62]{3,2,1,0:T(8,128)} %bitcast.18, f32[4,2,8,62]{3,2,1,0:T(8,128)} %bitcast.16), custom_call_target="tpu_custom_call" | custom-call | tf_op jit(solution)/shard_map/pallas_call | solution.py:512
  48.3 1.3 %copy.17 = f32[2,2,62,8]{2,3,1,0:T(8,128)} copy(f32[2,2,62,8]{2,3,1,0:T(8,128)} %bitcast.20) | data formatting | bytes 15872
  49.6 1.4 %copy.18 = f32[4,2,62,8]{2,3,1,0:T(8,128)} copy(f32[4,2,62,8]{2,3,1,0:T(8,128)} %bitcast.17) | data formatting | bytes 31744
  51.0 1.3 %copy.19 = f32[2,2,62,8]{2,3,1,0:T(8,128)} copy(f32[2,2,62,8]{2,3,1,0:T(8,128)} %bitcast.19) | data formatting | bytes 15872
where the time goes:
time: 52.7 us; the launch traced here: 52.3 us
  Pallas kernels  47.7 us (91%)
  local copies, waits for them, and re-layouts  4.02 us (8%)
  between operations  0.65 us (1%)
    pallas_call x1, Pallas kernels, finish(): pl.pallas_call(functools.partial(finish_kernel, chan_count, sub_count, ha...  18.9 us
    pallas_call x1, Pallas kernels, accumulate(): pl.pallas_call(kernel, grid_spec=pltpu.PrefetchScalarGridSpec(num_scalar_...  17.9 us
    pallas_call x1, Pallas kernels, gather_gains(): pl.pallas_call(functools.partial(gather_kernel, chan_count, sub_count, ha...  10.8 us
    unnamed x3, local copies, waits for them, and re-layouts  4.02 us

commit v1 on v0

v1 whole, which is shorter than its diff:
```python
import functools

import jax
import jax.numpy as jnp
import numpy as np
from jax import lax
from jax.experimental import pallas as pl
from jax.experimental.pallas import tpu as pltpu
from jax.sharding import PartitionSpec as P

LANES = 128
GROUP = 4
UNROLL = 20


def lay_pair(load, pad, half, width):
    total = None
    for part in range(half):
        block = load(part)
        pad[part % 2, :, : block.shape[1]] = block
        value = pad[part % 2]
        if part:
            value = pltpu.roll(value, part * width, axis=1)
        total = value if total is None else total + value
    return total


def basis_of(channel, channels):
    x = (2.0 * channel - (channels - 1)) / max(channels - 1, 1)
    return [
        jnp.ones_like(x),
        x,
        0.5 * (3.0 * x * x - 1.0),
        0.5 * (5.0 * x * x * x - 3.0 * x),
    ]


def inverse_gram(channels):
    f = np.arange(channels, dtype=np.float64)
    x = (2.0 * f - (channels - 1)) / max(channels - 1, 1)
    basis = np.stack([np.ones_like(x), x, 0.5 * (3 * x * x - 1), 0.5 * (5 * x * x * x - 3 * x)])
    return np.linalg.inv(basis @ basis.T)


def hermitian_rows(real, imag, upper, sign):
    half = real.shape[0] // 2
    groups_real = [real * real + imag * imag]
    groups_imag = []
    for shift in range(1, half + 1):
        turned_real = pltpu.roll(real, 2 * half - shift, axis=0)
        turned_imag = pltpu.roll(imag, 2 * half - shift, axis=0)
        groups_real.append(real * turned_real + imag * turned_imag)
        if sign > 0:
            groups_imag.append(real * turned_imag - imag * turned_real)
        else:
            groups_imag.append(imag * turned_real - real * turned_imag)
    mixed = jnp.where(upper, groups_real.pop(), groups_imag.pop())
    return groups_real + groups_imag + [mixed]


def solve_hermitian(groups_real, groups_imag, mixed, ridge, side_real, side_imag):
    directions = side_real.shape[0]
    middle = directions // 2
    row = lax.broadcasted_iota(jnp.int32, side_real.shape, 0)
    upper = row < middle
    swapped = pltpu.roll(mixed, middle, axis=0)
    real = {0: groups_real[0] + ridge, middle: jnp.where(upper, mixed, swapped)}
    imag = {0: jnp.zeros_like(ridge), middle: jnp.where(upper, -swapped, mixed)}
    for d in range(1, middle):
        real[d], imag[d] = groups_real[d], groups_imag[d - 1]
        real[directions - d] = pltpu.roll(groups_real[d], d, axis=0)
        imag[directions - d] = -pltpu.roll(groups_imag[d - 1], d, axis=0)
    columns = []
    for l in range(directions):
        column_real, column_imag = real[l], imag[l]
        for k in range(1, directions):
            here = row == k
            d = (l - k) % directions
            column_real = jnp.where(here, real[d], column_real)
            column_imag = jnp.where(here, imag[d], column_imag)
        columns.append((column_real, column_imag))
    columns.append((side_real, side_imag))
    scale = jnp.zeros_like(ridge)
    for j in range(directions):
        pivot_real, pivot_imag = columns[j]
        inverse = 1.0 / pivot_real[j : j + 1]
        here = row == j
        scale = jnp.where(here, jnp.broadcast_to(inverse, scale.shape), scale)
        factor_real = jnp.where(here, 0.0, pivot_real * inverse)
        factor_imag = jnp.where(here, 0.0, pivot_imag * inverse)
        for l in range(j + 1, directions + 1):
            value_real, value_imag = columns[l]
            head_real, head_imag = value_real[j : j + 1], value_imag[j : j + 1]
            columns[l] = (
                value_real - (factor_real * head_real - factor_imag * head_imag),
                value_imag - (factor_real * head_imag + factor_imag * head_real),
            )
    return columns[-1][0] * scale, columns[-1][1] * scale


def encode(sums, directions):
    normal_rows = directions * directions
    side = sums[normal_rows:]
    high = side.astype(jnp.bfloat16)
    low = (side - high.astype(jnp.float32)).astype(jnp.bfloat16)
    return jnp.concatenate([sums[:normal_rows].astype(jnp.bfloat16), high, low], axis=0)


def decode(coded, directions):
    wide = coded.astype(jnp.float32)
    normal_rows = directions * directions
    side_rows = 2 * directions
    high, low = wide[normal_rows : normal_rows + side_rows], wide[normal_rows + side_rows :]
    return jnp.concatenate([wide[:normal_rows], high + low], axis=0)


def sort_tiles(owner, channel, base, codes, owners, sub_count, half, groups, entries):
    tiles = owner.shape[1]
    slots = groups * GROUP
    sub = jnp.zeros_like(channel)
    for number in range(1, sub_count):
        sub = sub + jnp.where(channel >= number * half, 1, 0)
    place = channel - sub * half
    key = owner * sub_count + sub
    entry = base * half + place
    same = jnp.where(
        lax.broadcasted_iota(jnp.int32, (owners, tiles), 0) == jnp.broadcast_to(key, (owners, tiles)), 1.0, 0.0
    )
    same_b = same.astype(jnp.bfloat16)
    until = jnp.where(
        lax.broadcasted_iota(jnp.int32, (tiles, tiles), 0) <= lax.broadcasted_iota(jnp.int32, (tiles, tiles), 1),
        1.0,
        0.0,
    ).astype(jnp.bfloat16)
    nt = (((1,), (1,)), ((), ()))
    count = jnp.dot(same_b, until, preferred_element_type=jnp.float32)

    def pieces(value):
        return jnp.floor((value + float(GROUP - 1)) * (1.0 / GROUP))

    wide = (owners, LANES)
    used = pieces(jnp.broadcast_to(count[:, tiles - 1 : tiles], wide))
    square = (owners, owners)
    row, column = lax.broadcasted_iota(jnp.int32, square, 0), lax.broadcasted_iota(jnp.int32, square, 1)
    before = jnp.where(column < row, 1.0, 0.0).astype(jnp.bfloat16)
    start = jnp.dot(before, used.astype(jnp.bfloat16), preferred_element_type=jnp.float32)
    position = jnp.sum(same * (start[:, :1] * float(GROUP) + count), axis=0, keepdims=True) - 1.0
    left = tiles - lax.broadcasted_iota(jnp.int32, (1, tiles), 1)
    features = jnp.concatenate(
        [left & 255, lax.shift_right_logical(left, 8), entry, key, jnp.zeros((4, tiles), jnp.int32)], axis=0
    )
    chosen = jnp.where(
        lax.broadcasted_iota(jnp.int32, (slots, tiles), 0)
        == jnp.broadcast_to(position.astype(jnp.int32), (slots, tiles)),
        1.0,
        0.0,
    ).astype(jnp.bfloat16)
    sorted_features = lax.dot_general(
        features.astype(jnp.float32).astype(jnp.bfloat16), chosen, nt, preferred_element_type=jnp.float32
    )
    tile = float(tiles) - (sorted_features[0:1] + 256.0 * sorted_features[1:2])
    codes[0:1, :slots] = jnp.clip(tile.astype(jnp.int32), 0, tiles)
    codes[1:2, :slots] = jnp.clip(sorted_features[2:3].astype(jnp.int32), 0, entries - 1)
    codes[2:3, :slots] = jnp.clip(sorted_features[3:4].astype(jnp.int32), 0, owners - 1)
    spread = -(-groups // LANES) * LANES
    number = lax.broadcasted_iota(jnp.int32, (owners, spread), 1).astype(jnp.float32)
    first = (jnp.broadcast_to(start[:, :1], number.shape) == number) & (
        jnp.broadcast_to(used[:, :1], number.shape) > 0.5
    )
    carried = 1.0 - jnp.max(jnp.where(first, 1.0, 0.0), axis=0, keepdims=True)
    codes[3:4, :spread] = carried.astype(jnp.int32)
    used_row = pieces(lax.dot_general(jnp.ones((8, tiles), jnp.bfloat16), same_b, nt, preferred_element_type=jnp.float32))
    upto = jnp.where(row <= column, 1.0, 0.0).astype(jnp.bfloat16)
    end = jnp.dot(used_row.astype(jnp.bfloat16), upto, preferred_element_type=jnp.float32)
    last = jnp.where(used_row > 0.5, end, 0.0).astype(jnp.int32)
    codes[4:5, :owners] = jnp.clip(last[0:1], 0, groups)


def whole_kernel(
    chan_count,
    sub_count,
    half,
    groups,
    rho_ref,
    owner_hbm,
    channel_hbm,
    base_hbm,
    coupling_hbm,
    observed_hbm,
    keep_hbm,
    pairs_hbm,
    gains_hbm,
    duals_hbm,
    consensus_hbm,
    out_ref,
    owner_ref,
    channel_ref,
    base_ref,
    coupling_ref,
    observed_ref,
    keep_ref,
    pairs_ref,
    gains_ref,
    duals_ref,
    consensus_ref,
    gain_table,
    table,
    turned,
    stations_of,
    coupling_f,
    observed_f,
    lane_mask,
    codes_v,
    codes,
    sums_ref,
    pad,
    near_src,
    near_buf,
    send_buf,
    far_buf,
    weights,
    basis_buf,
    local_sem,
    gains_send,
    gains_recv,
    near_send,
    near_recv,
    far_send,
    far_recv,
    last_send,
    last_recv,
):
    chan, sub = lax.axis_index("chan"), lax.axis_index("sub")
    owners = chan_count * sub_count
    channels = owners * half
    width = LANES // half
    directions, stations = duals_ref.shape[2], duals_ref.shape[3]
    degree = consensus_ref.shape[0]
    tiles = keep_ref.shape[0]
    tile_rows = keep_ref.shape[1]
    bases = pairs_ref.shape[0]
    me = chan * sub_count + sub
    mesh_id = pl.DeviceIdType.MESH

    def device(flat):
        return {"chan": lax.div(flat, sub_count), "sub": lax.rem(flat, sub_count)}

    barrier = pltpu.get_barrier_semaphore()
    for offset in range(1, owners):
        pl.semaphore_signal(
            barrier, inc=1, device_id=device(lax.rem(me + offset, owners)), device_id_type=mesh_id
        )

    loads = []
    for number, (source, target) in enumerate(
        [
            (gains_hbm, gains_ref),
            (owner_hbm, owner_ref),
            (channel_hbm, channel_ref),
            (base_hbm, base_ref),
            (pairs_hbm, pairs_ref),
            (coupling_hbm, coupling_ref),
            (observed_hbm, observed_ref),
            (keep_hbm, keep_ref),
            (duals_hbm, duals_ref),
            (consensus_hbm, consensus_ref),
        ]
    ):
        copy = pltpu.make_async_copy(source, target, local_sem.at[number])
        copy.start()
        loads.append(copy)

    pad[...] = jnp.zeros_like(pad)
    loads[0].wait()
    for owner in range(sub_count):
        for part in range(2):
            gain_table[me - sub + owner, part] = lay_pair(
                lambda number: gains_ref[owner * half + number, part], pad, half, width
            )
    pl.semaphore_wait(barrier, owners - 1)
    gathers = []
    for offset in range(1, chan_count):
        mine_here = gain_table.at[pl.ds(chan * sub_count, sub_count)]
        copy = pltpu.make_async_remote_copy(
            src_ref=mine_here,
            dst_ref=mine_here,
            send_sem=gains_send.at[offset],
            recv_sem=gains_recv.at[offset],
            device_id={"chan": lax.rem(chan + offset, chan_count)},
            device_id_type=mesh_id,
        )
        copy.start()
        gathers.append(copy)

    for copy in loads[1:4]:
        copy.wait()
    codes_v[...] = jnp.zeros_like(codes_v)
    sort_tiles(owner_ref[...], channel_ref[...], base_ref[...], codes_v, owners, sub_count, half, groups, bases * half)
    to_scalar = pltpu.make_async_copy(codes_v, codes, local_sem.at[len(loads)])
    to_scalar.start()

    loads[4].wait()
    turned[...] = jnp.zeros_like(turned)
    for base in range(bases):
        both = pairs_ref[base]
        turned[2 * base : 2 * base + 2, :] = both.astype(jnp.float32)
        for part in range(half):
            stations_of[base * half + part] = both + part * width
    columns = jnp.transpose(turned[...])
    lane = lax.broadcasted_iota(jnp.int32, (tile_rows, LANES), 1).astype(jnp.float32)
    for base in range(bases):
        for end in range(2):
            station = jnp.broadcast_to(columns[:, 2 * base + end : 2 * base + end + 1], lane.shape)
            for part in range(half):
                table[base * half + part, end * tile_rows : (end + 1) * tile_rows, :] = jnp.where(
                    station == lane - float(part * width), 1.0, 0.0
                ).astype(jnp.bfloat16)

    for copy in loads[5:]:
        copy.wait()
    step_rows = 2 * directions

    def widen(step, carry):
        span = pl.ds(pl.multiple_of(step * 8 * step_rows, 8 * step_rows), 8 * step_rows)
        coupling_f[span, :] = coupling_ref[span, :].astype(jnp.float32)
        return carry

    lax.fori_loop(0, tiles // 8, widen, 0)
    coupling_f[tiles * step_rows :, :] = jnp.zeros((8 * step_rows, tile_rows), jnp.float32)
    observed_f[: 2 * tiles, :] = observed_ref[...].astype(jnp.float32)
    observed_f[2 * tiles :, :] = jnp.zeros((8, tile_rows), jnp.float32)
    lane_mask[:tiles, :] = jnp.where(keep_ref[...] > 0, 0, width - 1)
    lane_mask[tiles:, :] = jnp.zeros((8, tile_rows), jnp.int32)

    shape = (directions, LANES)
    row = lax.broadcasted_iota(jnp.int32, shape, 0)
    rho = jnp.zeros(shape, jnp.float32)
    for k in range(directions):
        rho = jnp.where(row == k, rho_ref[k], rho)
    place = lax.broadcasted_iota(jnp.int32, (owners, LANES), 1)
    of = lax.broadcasted_iota(jnp.int32, (owners, LANES), 0)
    everyone = basis_of((of * half + lax.div(place, width)).astype(jnp.float32), channels)
    for d in range(degree):
        basis_buf[d] = everyone[d]

    normal_rows = directions * directions
    out_rows = normal_rows + 2 * directions
    sums_ref[0] = jnp.zeros((out_rows, LANES), jnp.float32)
    upper = row < directions // 2
    to_scalar.wait()
    for copy in gathers:
        copy.wait_recv()

    def spread(values):
        return jnp.broadcast_to(values, shape)

    def pick(values, index):
        return jnp.take_along_axis(values, index, axis=1, mode="promise_in_bounds")

    def one_tile(slot):
        tile = jnp.clip(codes[0, slot], 0, tiles)
        entry = jnp.clip(codes[1, slot], 0, bases * half - 1)
        owner = jnp.clip(codes[2, slot], 0, owners - 1)
        first = tile * step_rows
        real = coupling_f[pl.ds(first, directions, stride=2), :]
        imag = coupling_f[pl.ds(first + 1, directions, stride=2), :]
        seen_real = spread(observed_f[pl.ds(2 * tile, 1), :])
        seen_imag = spread(observed_f[pl.ds(2 * tile + 1, 1), :])
        masked = spread(lane_mask[pl.ds(tile, 1), :])
        near = spread(stations_of[entry, pl.ds(0, 1), :]) | masked
        far = spread(stations_of[entry, pl.ds(1, 1), :]) | masked
        gain_real, gain_imag = gain_table[owner, 0], gain_table[owner, 1]
        near_real, near_imag = pick(gain_real, near), pick(gain_imag, near)
        far_real, far_imag = pick(gain_real, far), pick(gain_imag, far)
        slope_real = real * far_real + imag * far_imag
        slope_imag = imag * far_real - real * far_imag
        other_real = real * near_real - imag * near_imag
        other_imag = real * near_imag + imag * near_real
        near_rows = hermitian_rows(slope_real, slope_imag, upper, 1) + [
            slope_real * seen_real + slope_imag * seen_imag,
            slope_real * seen_imag - slope_imag * seen_real,
        ]
        far_rows = hermitian_rows(other_real, other_imag, upper, -1) + [
            other_real * seen_real + other_imag * seen_imag,
            other_imag * seen_real - other_real * seen_imag,
        ]
        rows = jnp.concatenate(
            [
                jnp.concatenate(near_rows, axis=0).astype(jnp.bfloat16),
                jnp.concatenate(far_rows, axis=0).astype(jnp.bfloat16),
            ],
            axis=1,
        )
        return jnp.dot(rows, table[entry], preferred_element_type=jnp.float32)

    def some_groups(step, carry):
        base_group = step * UNROLL
        running = sums_ref[base_group]
        for number in range(UNROLL):
            group = base_group + number
            total = one_tile(group * GROUP)
            for inner in range(1, GROUP):
                total = total + one_tile(group * GROUP + inner)
            running = running * codes[3, group].astype(jnp.float32) + total
            sums_ref[group + 1] = running
        return carry

    lax.fori_loop(0, groups // UNROLL, some_groups, 0)

    def sums_of(owner):
        return sums_ref[jnp.clip(codes[4, owner], 0, groups)]

    near = {}
    order = list(range(1, chan_count)) + [0]
    for offset in order:
        target = lax.rem(chan + offset, chan_count)
        for shift in range(1, sub_count):
            other = lax.rem(sub + shift, sub_count)
            near_src[shift - 1, offset] = encode(sums_of(target * sub_count + other), directions)
            copy = pltpu.make_async_remote_copy(
                src_ref=near_src.at[shift - 1, offset],
                dst_ref=near_buf.at[shift - 1, offset],
                send_sem=near_send.at[shift - 1, offset],
                recv_sem=near_recv.at[shift - 1, offset],
                device_id={"sub": other},
                device_id_type=mesh_id,
            )
            copy.start()
            near[offset, shift] = copy

    mine = [jnp.broadcast_to(basis_buf[d, pl.ds(me, 1), :], shape) for d in range(degree)]
    duals = [
        lay_pair(lambda number: duals_ref[number, part], pad, half, width) for part in range(2)
    ]
    anchors = []
    for part in range(2):
        anchor = jnp.zeros(shape, jnp.float32)
        for d in range(degree):
            anchor = anchor + mine[d] * lay_pair(
                lambda number: consensus_ref[d, part], pad, half, width
            )
        anchors.append(anchor)

    far = []
    for offset in order:
        target = lax.rem(chan + offset, chan_count)
        total = sums_of(target * sub_count + sub)
        for shift in range(1, sub_count):
            near[offset, shift].wait_recv()
            total = total + decode(near_buf[shift - 1, offset], directions)
        if offset:
            send_buf[offset] = encode(total, directions)
            copy = pltpu.make_async_remote_copy(
                src_ref=send_buf.at[offset],
                dst_ref=far_buf.at[offset],
                send_sem=far_send.at[offset],
                recv_sem=far_recv.at[offset],
                device_id={"chan": target},
                device_id_type=mesh_id,
            )
            copy.start()
            far.append((offset, copy))
    for offset, copy in far:
        copy.wait_recv()
        total = total + decode(far_buf[offset], directions)

    middle = directions // 2
    group = [total[i * directions : (i + 1) * directions] for i in range(directions + 2)]
    solved = solve_hermitian(
        group[:middle],
        group[middle : directions - 1],
        group[directions - 1],
        rho,
        group[directions] - duals[0] + rho * anchors[0],
        group[directions + 1] - duals[1] + rho * anchors[1],
    )
    weights[me] = jnp.concatenate(
        [solved[part] + duals[part] / rho for part in range(2)], axis=0
    ).astype(jnp.bfloat16)

    last = []
    for offset in range(1, owners):
        copy = pltpu.make_async_remote_copy(
            src_ref=weights.at[me],
            dst_ref=weights.at[me],
            send_sem=last_send.at[offset],
            recv_sem=last_recv.at[offset],
            device_id=device(lax.rem(me + offset, owners)),
            device_id_type=mesh_id,
        )
        copy.start()
        last.append(copy)

    def store(first, part, value):
        for number in range(half):
            out_ref[first + number, part] = (
                pltpu.roll(value, LANES - number * width, axis=1) if number else value
            )

    for part in range(2):
        store(0, part, solved[part])
    for copy in last:
        copy.wait_recv()
    inverse = inverse_gram(channels)
    totals = []
    for d in range(degree):
        value = jnp.zeros((2 * directions, LANES), jnp.float32)
        for number in range(owners):
            value = value + basis_buf[d, number : number + 1, :] * weights[number].astype(jnp.float32)
        folded = value
        for number in range(1, half):
            folded = folded + pltpu.roll(value, number * width, axis=1)
        totals.append(folded)
    fitted = jnp.zeros((2 * directions, LANES), jnp.float32)
    for d in range(degree):
        value = sum(float(inverse[d, e]) * totals[e] for e in range(degree))
        for part in range(2):
            out_ref[half + d, part] = value[part * directions : (part + 1) * directions]
        fitted = fitted + jnp.concatenate([mine[d], mine[d]], axis=0) * value
    for part in range(2):
        fit = fitted[part * directions : (part + 1) * directions]
        store(half + degree, part, duals[part] + rho * (solved[part] - fit))
    for copy in gathers:
        copy.wait_send()
    for copy in near.values():
        copy.wait_send()
    for _, copy in far:
        copy.wait_send()
    for copy in last:
        copy.wait_send()


def deliver_kernel(result_ref, gains_out, consensus_out, duals_out):
    first = 0
    for ref in (gains_out, consensus_out, duals_out):
        count, _, _, stations = ref.shape
        for number in range(count):
            ref[number] = result_ref[first + number][:, :, :stations]
        first += count


def body(
    predicted_sky_response,
    measured_correlation,
    keep_indicator,
    tile_owner,
    tile_channel,
    tile_base,
    pairs,
    gains,
    duals,
    consensus,
    rho,
):
    channels_here, _, stations, directions = gains.shape
    chan_count = lax.axis_size("chan")
    sub_count = lax.axis_size("sub")
    half = channels_here // sub_count
    owners = chan_count * sub_count
    tiles, _, _, tile_rows = predicted_sky_response.shape
    bases = pairs.shape[0]
    degree = consensus.shape[0]
    width = LANES // half
    if width & (width - 1) or stations >= width or tile_rows != LANES:
        raise ValueError("unsupported sizes")
    groups = -(-(tiles + owners * (GROUP - 1)) // GROUP)
    groups = -(-groups // UNROLL) * UNROLL
    code_width = -(-max(groups * GROUP, owners) // LANES) * LANES
    out_rows = directions * directions + 2 * directions
    coded = out_rows + 2 * directions
    gains_t = jnp.swapaxes(gains, 2, 3)
    duals_t = jnp.swapaxes(duals, 2, 3)
    consensus_t = jnp.swapaxes(consensus, 2, 3)
    operands = [
        tile_owner.reshape(1, tiles),
        tile_channel.reshape(1, tiles),
        tile_base.reshape(1, tiles),
        predicted_sky_response.reshape(tiles * 2 * directions, tile_rows),
        measured_correlation.reshape(tiles * 2, tile_rows),
        keep_indicator,
        pairs,
        gains_t,
        duals_t,
        consensus_t,
    ]
    vmem, dma = pltpu.VMEM, pltpu.SemaphoreType.DMA
    f32, bf16, i32 = jnp.float32, jnp.bfloat16, jnp.int32
    result = pl.pallas_call(
        functools.partial(whole_kernel, chan_count, sub_count, half, groups),
        out_shape=jax.ShapeDtypeStruct((2 * half + degree, 2, directions, LANES), f32),
        in_specs=[pl.BlockSpec(memory_space=pltpu.SMEM)]
        + [pl.BlockSpec(memory_space=pl.ANY)] * len(operands),
        out_specs=pl.BlockSpec(memory_space=pltpu.VMEM),
        scratch_shapes=[vmem(x.shape, x.dtype) for x in operands]
        + [
            vmem((owners, 2, directions, LANES), f32),
            vmem((bases * half, 2 * tile_rows, LANES), bf16),
            vmem((LANES, tile_rows), f32),
            vmem((bases * half, 2, tile_rows), i32),
            vmem(((tiles + 8) * 2 * directions, tile_rows), f32),
            vmem((2 * tiles + 8, tile_rows), f32),
            vmem((tiles + 8, tile_rows), i32),
            vmem((8, code_width), i32),
            pltpu.SMEM((8, code_width), i32),
            vmem((groups + 1, out_rows, LANES), f32),
            vmem((2, directions, LANES), f32),
            vmem((sub_count - 1, chan_count, coded, LANES), bf16),
            vmem((sub_count - 1, chan_count, coded, LANES), bf16),
            vmem((chan_count, coded, LANES), bf16),
            vmem((chan_count, coded, LANES), bf16),
            vmem((owners, 2 * directions, LANES), bf16),
            vmem((degree, owners, LANES), f32),
            dma((len(operands) + 1,)),
            dma((chan_count,)),
            dma((chan_count,)),
            dma((sub_count - 1, chan_count)),
            dma((sub_count - 1, chan_count)),
            dma((chan_count,)),
            dma((chan_count,)),
            dma((owners,)),
            dma((owners,)),
        ],
        compiler_params=pltpu.CompilerParams(
            collective_id=1, has_side_effects=True, vmem_limit_bytes=60 << 20
        ),
    )(rho, *[operands[i] for i in range(len(operands))])
    outputs = pl.pallas_call(
        deliver_kernel,
        out_shape=tuple(
            jax.ShapeDtypeStruct(x.shape, f32) for x in (duals_t, consensus_t, duals_t)
        ),
        in_specs=[pl.BlockSpec(memory_space=pltpu.VMEM)],
        out_specs=tuple(pl.BlockSpec(memory_space=pltpu.VMEM) for _ in range(3)),
    )(result)
    return tuple(jnp.swapaxes(x, 2, 3) for x in outputs)


def solution(mesh):
    placed = (
        P(("groups", "chan", "sub"), None, None, None),
        P(("groups", "chan", "sub"), None, None),
        P(("groups", "chan", "sub"), None),
        P(("groups", "chan", "sub"), None),
        P(("groups", "chan", "sub")),
        P(("groups", "chan", "sub")),
        P(),
        P(("groups", "chan"), None, None, None),
        P(("groups", "chan", "sub"), None, None, None),
        P("groups", None, None, None),
        P(),
    )
    return jax.shard_map(
        body,
        mesh=mesh,
        in_specs=placed,
        out_specs=(
            P(("groups", "chan", "sub"), None, None, None),
            P("groups", None, None, None),
            P(("groups", "chan", "sub"), None, None, None),
        ),
        check_vma=False,
    )
```

time: 52.7 us -> 40.2 us (0.76)
  Pallas kernels: 47.7 us -> 39.3 us
  local copies, waits for them, and re-layouts: 4.02 us -> 0 us
    pallas_call x3 -> x2, Pallas kernels: 47.7 us -> 39.3 us  [the longest x1 37.9 us: body(): pl.pallas_call(functools.partial(whole_kernel, chan_count, sub_count, hal...]
    unnamed x3 -> x0, local copies, waits for them, and re-layouts: 4.02 us -> none
where the time goes in v1:
time: 40.2 us; the launch traced here: 40 us
  Pallas kernels  39.3 us (98%)
  between operations  0.64 us (2%)
    pallas_call x1, Pallas kernels, body(): pl.pallas_call(functools.partial(whole_kernel, chan_count, sub_count, hal...  37.9 us
    pallas_call x1, Pallas kernels, body(): pl.pallas_call(deliver_kernel, out_shape=tuple((jax.ShapeDtypeStruct(x.sh...  1.47 us

profile of v1, /device:TPU:0, one launch (start us, length us, event | category | flops | bytes accessed | tf_op | source)
XLA Modules:
  0.0 40.0 jit_solution(10314143321652162963)
XLA Ops:
  0.6 37.9 %shard_map.130.result_ref = f32[8,2,8,128]{3,2,1,0:T(8,128)} custom-call(f32[8]{0:T(128)} %rho_ref.1, s32[1,512]{1,0:T(1,128)} %bitcast.16, s32[1,512]{1,0:T(1,128)} %bitcast.17, s32[1,512]{1,0:T(1,128)} %bitcast.18, bf16[8192,128]{1,0:T(8,128)(2,1)} %bitcast.11, bf16[1024,128]{1,0:T(8,128)(2,1)} %bitcast.12, s32[512,128]{1,0:T(8,128)} %keep_hbm.1, ...), custom_call_target="tpu_custom_call" | custom-call | tf_op jit(solution)/shard_map/pallas_call | solution.py:588
  38.5 1.5 %shard_map.131 = (f32[2,2,8,62]{3,2,1,0:T(8,128)}, f32[4,2,8,62]{3,2,1,0:T(8,128)}, f32[2,2,8,62]{3,2,1,0:T(8,128)}) custom-call(f32[8,2,8,128]{3,2,1,0:T(8,128)} %shard_map.130.result_ref), custom_call_target="tpu_custom_call" | custom-call | tf_op jit(solution)/shard_map/pallas_call | solution.py:627

commit v2 on v1

--- a/solution.py
+++ b/solution.py
@@ -42,20 +42,38 @@
     return np.linalg.inv(basis @ basis.T)
 
 
-def hermitian_rows(real, imag, upper, sign):
-    half = real.shape[0] // 2
-    groups_real = [real * real + imag * imag]
-    groups_imag = []
-    for shift in range(1, half + 1):
-        turned_real = pltpu.roll(real, 2 * half - shift, axis=0)
-        turned_imag = pltpu.roll(imag, 2 * half - shift, axis=0)
-        groups_real.append(real * turned_real + imag * turned_imag)
-        if sign > 0:
-            groups_imag.append(real * turned_imag - imag * turned_real)
-        else:
-            groups_imag.append(imag * turned_real - real * turned_imag)
-    mixed = jnp.where(upper, groups_real.pop(), groups_imag.pop())
-    return groups_real + groups_imag + [mixed]
+def end_rows(real, imag, seen_real, seen_imag, upper, sign, turn):
+    directions = real.shape[0]
+    bf16 = jnp.bfloat16
+    flipped = -real if sign > 0 else -imag
+    for number, value in enumerate((real, imag, flipped)):
+        turn[number, :directions, :] = value
+        turn[number, directions:, :] = value
+
+    def turned(number, shift):
+        return turn[number, shift : shift + directions, :]
+
+    def pair(first, second):
+        return jnp.concatenate([first, second], axis=0).astype(bf16)
+
+    left, right = pair(real, real), pair(imag, imag)
+    ahead_real, ahead_imag = pair(turned(0, 1), turned(0, 2)), pair(turned(1, 1), turned(1, 2))
+    both = left * ahead_real + right * ahead_imag
+    cross = left * ahead_imag - right * ahead_real if sign > 0 else right * ahead_real - left * ahead_imag
+    if sign > 0:
+        cross_left, cross_right = (turned(1, 3), turned(1, 4)), (turned(2, 3), turned(2, 4))
+    else:
+        cross_left, cross_right = (turned(2, 3), turned(2, 4)), (turned(0, 3), turned(0, 4))
+    mixed_left = jnp.where(upper, turned(0, 4), cross_left[1])
+    mixed_right = jnp.where(upper, turned(1, 4), cross_right[1])
+    third = left * pair(turned(0, 3), mixed_left) + right * pair(turned(1, 3), mixed_right)
+    last = left * pair(cross_left[0], real) + right * pair(cross_right[0], imag)
+    side_real = real * seen_real + imag * seen_imag
+    if sign > 0:
+        side_imag = real * seen_imag - imag * seen_real
+    else:
+        side_imag = imag * seen_real - real * seen_imag
+    return jnp.concatenate([both, cross, third, last, pair(side_real, side_imag)], axis=0)
 
 
 def solve_hermitian(groups_real, groups_imag, mixed, ridge, side_real, side_imag):
@@ -213,6 +231,7 @@
     codes_v,
     codes,
     sums_ref,
+    turn,
     pad,
     near_src,
     near_buf,
@@ -355,9 +374,21 @@
         return jnp.broadcast_to(values, shape)
 
     def pick(values, index):
-        return jnp.take_along_axis(values, index, axis=1, mode="promise_in_bounds")
-
-    def one_tile(slot):
+        return lax.gather(
+            values,
+            index[..., None],
+            lax.GatherDimensionNumbers(
+                offset_dims=(),
+                collapsed_slice_dims=(1,),
+                start_index_map=(1,),
+                operand_batching_dims=(0,),
+                start_indices_batching_dims=(0,),
+            ),
+            slice_sizes=(1, 1),
+            mode=lax.GatherScatterMode.PROMISE_IN_BOUNDS,
+        )
+
+    def one_tile(slot, spot):
         tile = jnp.clip(codes[0, slot], 0, tiles)
         entry = jnp.clip(codes[1, slot], 0, bases * half - 1)
         owner = jnp.clip(codes[2, slot], 0, owners - 1)
@@ -376,31 +407,26 @@
         slope_imag = imag * far_real - real * far_imag
         other_real = real * near_real - imag * near_imag
         other_imag = real * near_imag + imag * near_real
-        near_rows = hermitian_rows(slope_real, slope_imag, upper, 1) + [
-            slope_real * seen_real + slope_imag * seen_imag,
-            slope_real * seen_imag - slope_imag * seen_real,
-        ]
-        far_rows = hermitian_rows(other_real, other_imag, upper, -1) + [
-            other_real * seen_real + other_imag * seen_imag,
-            other_imag * seen_real - other_real * seen_imag,
-        ]
-        rows = jnp.concatenate(
-            [
-                jnp.concatenate(near_rows, axis=0).astype(jnp.bfloat16),
-                jnp.concatenate(far_rows, axis=0).astype(jnp.bfloat16),
-            ],
-            axis=1,
-        )
-        return jnp.dot(rows, table[entry], preferred_element_type=jnp.float32)
+        return [
+            end_rows(slope_real, slope_imag, seen_real, seen_imag, upper, 1, turn.at[2 * spot]),
+            end_rows(other_real, other_imag, seen_real, seen_imag, upper, -1, turn.at[2 * spot + 1]),
+        ], table[entry]
 
     def some_groups(step, carry):
         base_group = step * UNROLL
         running = sums_ref[base_group]
         for number in range(UNROLL):
             group = base_group + number
-            total = one_tile(group * GROUP)
-            for inner in range(1, GROUP):
-                total = total + one_tile(group * GROUP + inner)
+            rows, entries = [], []
+            for inner in range(GROUP):
+                ends, entry = one_tile(group * GROUP + inner, number * GROUP + inner)
+                rows += ends
+                entries.append(entry)
+            total = jnp.dot(
+                jnp.concatenate(rows, axis=1),
+                jnp.concatenate(entries, axis=0),
+                preferred_element_type=jnp.float32,
+            )
             running = running * codes[3, group].astype(jnp.float32) + total
             sums_ref[group + 1] = running
         return carry
@@ -464,12 +490,11 @@
         copy.wait_recv()
         total = total + decode(far_buf[offset], directions)
 
-    middle = directions // 2
     group = [total[i * directions : (i + 1) * directions] for i in range(directions + 2)]
     solved = solve_hermitian(
-        group[:middle],
-        group[middle : directions - 1],
-        group[directions - 1],
+        [group[7], group[0], group[1], group[4]],
+        [group[2], group[3], group[6]],
+        group[5],
         rho,
         group[directions] - duals[0] + rho * anchors[0],
         group[directions + 1] - duals[1] + rho * anchors[1],
@@ -561,7 +586,7 @@
     bases = pairs.shape[0]
     degree = consensus.shape[0]
     width = LANES // half
-    if width & (width - 1) or stations >= width or tile_rows != LANES:
+    if width & (width - 1) or stations >= width or tile_rows != LANES or directions != 8:
         raise ValueError("unsupported sizes")
     groups = -(-(tiles + owners * (GROUP - 1)) // GROUP)
     groups = -(-groups // UNROLL) * UNROLL
@@ -603,6 +628,7 @@
             vmem((8, code_width), i32),
             pltpu.SMEM((8, code_width), i32),
             vmem((groups + 1, out_rows, LANES), f32),
+            vmem((2 * GROUP * UNROLL, 3, 2 * directions, LANES), f32),
             vmem((2, directions, LANES), f32),
             vmem((sub_count - 1, chan_count, coded, LANES), bf16),
             vmem((sub_count - 1, chan_count, coded, LANES), bf16),

time: 40.2 us -> 39.2 us (0.975)
  Pallas kernels: 39.3 us -> 38.4 us
    pallas_call x1, Pallas kernels: 37.9 us -> 36.9 us  [body(): pl.pallas_call(functools.partial(whole_kernel, chan_count, sub_count, hal...]
where the time goes in v2:
time: 39.2 us; the launch traced here: 39 us
  Pallas kernels  38.4 us (98%)
  between operations  0.64 us (2%)
    pallas_call x1, Pallas kernels, body(): pl.pallas_call(functools.partial(whole_kernel, chan_count, sub_count, hal...  36.9 us
    pallas_call x1, Pallas kernels, body(): pl.pallas_call(deliver_kernel, out_shape=tuple((jax.ShapeDtypeStruct(x.sh...  1.47 us

profile of v2, /device:TPU:0, one launch (start us, length us, event | category | flops | bytes accessed | tf_op | source)
XLA Modules:
  0.0 39.0 jit_solution(8816386516259256659)
XLA Ops:
  0.6 36.9 %shard_map.130.result_ref = f32[8,2,8,128]{3,2,1,0:T(8,128)} custom-call(f32[8]{0:T(128)} %rho_ref.1, s32[1,512]{1,0:T(1,128)} %bitcast.16, s32[1,512]{1,0:T(1,128)} %bitcast.17, s32[1,512]{1,0:T(1,128)} %bitcast.18, bf16[8192,128]{1,0:T(8,128)(2,1)} %bitcast.11, bf16[1024,128]{1,0:T(8,128)(2,1)} %bitcast.12, s32[512,128]{1,0:T(8,128)} %keep_hbm.1, ...), custom_call_target="tpu_custom_call" | custom-call | tf_op jit(solution)/shard_map/pallas_call | solution.py:613
  37.6 1.5 %shard_map.131 = (f32[2,2,8,62]{3,2,1,0:T(8,128)}, f32[4,2,8,62]{3,2,1,0:T(8,128)}, f32[2,2,8,62]{3,2,1,0:T(8,128)}) custom-call(f32[8,2,8,128]{3,2,1,0:T(8,128)} %shard_map.130.result_ref), custom_call_target="tpu_custom_call" | custom-call | tf_op jit(solution)/shard_map/pallas_call | solution.py:653

commit v3 on v2

--- a/solution.py
+++ b/solution.py
@@ -42,16 +42,12 @@
     return np.linalg.inv(basis @ basis.T)
 
 
-def end_rows(real, imag, seen_real, seen_imag, upper, sign, turn):
+def end_rows(real, imag, seen_real, seen_imag, upper, sign):
     directions = real.shape[0]
     bf16 = jnp.bfloat16
     flipped = -real if sign > 0 else -imag
-    for number, value in enumerate((real, imag, flipped)):
-        turn[number, :directions, :] = value
-        turn[number, directions:, :] = value
-
     def turned(number, shift):
-        return turn[number, shift : shift + directions, :]
+        return pltpu.roll((real, imag, flipped)[number], directions - shift, axis=0)
 
     def pair(first, second):
         return jnp.concatenate([first, second], axis=0).astype(bf16)
@@ -132,14 +128,14 @@
     return jnp.concatenate([wide[:normal_rows], high + low], axis=0)
 
 
-def sort_tiles(owner, channel, base, codes, owners, sub_count, half, groups, entries):
-    tiles = owner.shape[1]
+def sort_tiles(rank, channel, base, codes, owners, sub_count, half, groups, entries):
+    tiles = rank.shape[1]
     slots = groups * GROUP
     sub = jnp.zeros_like(channel)
     for number in range(1, sub_count):
         sub = sub + jnp.where(channel >= number * half, 1, 0)
     place = channel - sub * half
-    key = owner * sub_count + sub
+    key = rank * sub_count + sub
     entry = base * half + place
     same = jnp.where(
         lax.broadcasted_iota(jnp.int32, (owners, tiles), 0) == jnp.broadcast_to(key, (owners, tiles)), 1.0, 0.0
@@ -226,12 +222,12 @@
     turned,
     stations_of,
     coupling_f,
+    coupling_t,
     observed_f,
     lane_mask,
     codes_v,
     codes,
     sums_ref,
-    turn,
     pad,
     near_src,
     near_buf,
@@ -261,8 +257,20 @@
     me = chan * sub_count + sub
     mesh_id = pl.DeviceIdType.MESH
 
+    top = chan_count - 1
+
     def device(flat):
         return {"chan": lax.div(flat, sub_count), "sub": lax.rem(flat, sub_count)}
+
+    def partner(rank):
+        flips, result, bit = top - rank, chan, 1
+        while bit < chan_count:
+            if flips & bit:
+                result = result + bit * (1 - 2 * lax.rem(lax.div(chan, bit), 2))
+            bit *= 2
+        return result
+
+    partners = [partner(rank) for rank in range(chan_count)]
 
     barrier = pltpu.get_barrier_semaphore()
     for offset in range(1, owners):
@@ -293,19 +301,18 @@
     loads[0].wait()
     for owner in range(sub_count):
         for part in range(2):
-            gain_table[me - sub + owner, part] = lay_pair(
+            gain_table[top * sub_count + owner, part] = lay_pair(
                 lambda number: gains_ref[owner * half + number, part], pad, half, width
             )
     pl.semaphore_wait(barrier, owners - 1)
     gathers = []
-    for offset in range(1, chan_count):
-        mine_here = gain_table.at[pl.ds(chan * sub_count, sub_count)]
+    for rank in range(top):
         copy = pltpu.make_async_remote_copy(
-            src_ref=mine_here,
-            dst_ref=mine_here,
-            send_sem=gains_send.at[offset],
-            recv_sem=gains_recv.at[offset],
-            device_id={"chan": lax.rem(chan + offset, chan_count)},
+            src_ref=gain_table.at[pl.ds(top * sub_count, sub_count)],
+            dst_ref=gain_table.at[pl.ds(rank * sub_count, sub_count)],
+            send_sem=gains_send.at[rank],
+            recv_sem=gains_recv.at[rank],
+            device_id={"chan": partners[rank]},
             device_id_type=mesh_id,
         )
         copy.start()
@@ -314,7 +321,9 @@
     for copy in loads[1:4]:
         copy.wait()
     codes_v[...] = jnp.zeros_like(codes_v)
-    sort_tiles(owner_ref[...], channel_ref[...], base_ref[...], codes_v, owners, sub_count, half, groups, bases * half)
+    named = owner_ref[...]
+    rank_of = top - (named + chan - 2 * (named & chan))
+    sort_tiles(rank_of, channel_ref[...], base_ref[...], codes_v, owners, sub_count, half, groups, bases * half)
     to_scalar = pltpu.make_async_copy(codes_v, codes, local_sem.at[len(loads)])
     to_scalar.start()
 
@@ -341,11 +350,14 @@
 
     def widen(step, carry):
         span = pl.ds(pl.multiple_of(step * 8 * step_rows, 8 * step_rows), 8 * step_rows)
-        coupling_f[span, :] = coupling_ref[span, :].astype(jnp.float32)
+        coupling_t[...] = coupling_ref[span, :].astype(jnp.float32)
+        for number in range(2):
+            value = coupling_t[pl.ds(number, 8 * directions, stride=2), :]
+            coupling_f[number, pl.ds(step * 8, 8)] = value.reshape(8, directions, tile_rows)
         return carry
 
     lax.fori_loop(0, tiles // 8, widen, 0)
-    coupling_f[tiles * step_rows :, :] = jnp.zeros((8 * step_rows, tile_rows), jnp.float32)
+    coupling_f[:, tiles:] = jnp.zeros((2, 1, directions, tile_rows), jnp.float32)
     observed_f[: 2 * tiles, :] = observed_ref[...].astype(jnp.float32)
     observed_f[2 * tiles :, :] = jnp.zeros((8, tile_rows), jnp.float32)
     lane_mask[:tiles, :] = jnp.where(keep_ref[...] > 0, 0, width - 1)
@@ -388,13 +400,11 @@
             mode=lax.GatherScatterMode.PROMISE_IN_BOUNDS,
         )
 
-    def one_tile(slot, spot):
+    def one_tile(slot):
         tile = jnp.clip(codes[0, slot], 0, tiles)
         entry = jnp.clip(codes[1, slot], 0, bases * half - 1)
         owner = jnp.clip(codes[2, slot], 0, owners - 1)
-        first = tile * step_rows
-        real = coupling_f[pl.ds(first, directions, stride=2), :]
-        imag = coupling_f[pl.ds(first + 1, directions, stride=2), :]
+        real, imag = coupling_f[0, tile], coupling_f[1, tile]
         seen_real = spread(observed_f[pl.ds(2 * tile, 1), :])
         seen_imag = spread(observed_f[pl.ds(2 * tile + 1, 1), :])
         masked = spread(lane_mask[pl.ds(tile, 1), :])
@@ -408,18 +418,67 @@
         other_real = real * near_real - imag * near_imag
         other_imag = real * near_imag + imag * near_real
         return [
-            end_rows(slope_real, slope_imag, seen_real, seen_imag, upper, 1, turn.at[2 * spot]),
-            end_rows(other_real, other_imag, seen_real, seen_imag, upper, -1, turn.at[2 * spot + 1]),
+            end_rows(slope_real, slope_imag, seen_real, seen_imag, upper, 1),
+            end_rows(other_real, other_imag, seen_real, seen_imag, upper, -1),
         ], table[entry]
 
+    def sums_of(rank, which):
+        return sums_ref[jnp.clip(codes[4, rank * sub_count + which], 0, groups)]
+
+    def near_copy(rank, shift):
+        return pltpu.make_async_remote_copy(
+            src_ref=near_src.at[shift - 1, rank],
+            dst_ref=near_buf.at[shift - 1, rank],
+            send_sem=near_send.at[shift - 1, rank],
+            recv_sem=near_recv.at[shift - 1, rank],
+            device_id={"sub": lax.rem(sub + shift, sub_count)},
+            device_id_type=mesh_id,
+        )
+
+    def far_copy(rank):
+        return pltpu.make_async_remote_copy(
+            src_ref=send_buf.at[rank],
+            dst_ref=far_buf.at[rank],
+            send_sem=far_send.at[rank],
+            recv_sem=far_recv.at[rank],
+            device_id={"chan": partners[rank]},
+            device_id_type=mesh_id,
+        )
+
+    def start_near(rank):
+        for shift in range(1, sub_count):
+            near_src[shift - 1, rank] = encode(sums_of(rank, lax.rem(sub + shift, sub_count)), directions)
+            near_copy(rank, shift).start()
+
+    def add_near(rank):
+        total = sums_of(rank, sub)
+        for shift in range(1, sub_count):
+            near_copy(rank, shift).wait_recv()
+            total = total + decode(near_buf[shift - 1, rank], directions)
+        return total
+
+    def start_far(rank):
+        send_buf[rank] = encode(add_near(rank), directions)
+        far_copy(rank).start()
+
     def some_groups(step, carry):
+        for rank, ready in enumerate(early):
+
+            @pl.when(step == ready)
+            def _():
+                start_near(rank)
+
+            @pl.when(step == ready + 1)
+            def _():
+                start_far(rank)
+
         base_group = step * UNROLL
         running = sums_ref[base_group]
         for number in range(UNROLL):
             group = base_group + number
             rows, entries = [], []
             for inner in range(GROUP):
-                ends, entry = one_tile(group * GROUP + inner, number * GROUP + inner)
+                ends, entry = one_tile(group * GROUP + inner)
                 rows += ends
                 entries.append(entry)
             total = jnp.dot(
@@ -431,28 +490,17 @@
             sums_ref[group + 1] = running
         return carry
 
-    lax.fori_loop(0, groups // UNROLL, some_groups, 0)
-
-    def sums_of(owner):
-        return sums_ref[jnp.clip(codes[4, owner], 0, groups)]
-
-    near = {}
-    order = list(range(1, chan_count)) + [0]
-    for offset in order:
-        target = lax.rem(chan + offset, chan_count)
-        for shift in range(1, sub_count):
-            other = lax.rem(sub + shift, sub_count)
-            near_src[shift - 1, offset] = encode(sums_of(target * sub_count + other), directions)
-            copy = pltpu.make_async_remote_copy(
-                src_ref=near_src.at[shift - 1, offset],
-                dst_ref=near_buf.at[shift - 1, offset],
-                send_sem=near_send.at[shift - 1, offset],
-                recv_sem=near_recv.at[shift - 1, offset],
-                device_id={"sub": other},
-                device_id_type=mesh_id,
-            )
-            copy.start()
-            near[offset, shift] = copy
+    steps = groups // UNROLL
+    most = 3 * tiles // chan_count + sub_count * (GROUP - 1)
+    early = []
+    for rank in range(top):
+        ready = -(-(rank + 1) * most // (GROUP * UNROLL))
+        if ready + 1 < steps:
+            early.append(ready)
+    lax.fori_loop(0, steps, some_groups, 0)
+
+    for rank in range(len(early), chan_count):
+        start_near(rank)
 
     mine = [jnp.broadcast_to(basis_buf[d, pl.ds(me, 1), :], shape) for d in range(degree)]
     duals = [
@@ -467,28 +515,12 @@
             )
         anchors.append(anchor)
 
-    far = []
-    for offset in order:
-        target = lax.rem(chan + offset, chan_count)
-        total = sums_of(target * sub_count + sub)
-        for shift in range(1, sub_count):
-            near[offset, shift].wait_recv()
-            total = total + decode(near_buf[shift - 1, offset], directions)
-        if offset:
-            send_buf[offset] = encode(total, directions)
-            copy = pltpu.make_async_remote_copy(
-                src_ref=send_buf.at[offset],
-                dst_ref=far_buf.at[offset],
-                send_sem=far_send.at[offset],
-                recv_sem=far_recv.at[offset],
-                device_id={"chan": target},
-                device_id_type=mesh_id,
-            )
-            copy.start()
-            far.append((offset, copy))
-    for offset, copy in far:
-        copy.wait_recv()
-        total = total + decode(far_buf[offset], directions)
+    for rank in range(len(early), top):
+        start_far(rank)
+    total = add_near(top)
+    for rank in range(top):
+        far_copy(rank).wait_recv()
+        total = total + decode(far_buf[rank], directions)
 
     group = [total[i * directions : (i + 1) * directions] for i in range(directions + 2)]
     solved = solve_hermitian(
@@ -504,17 +536,21 @@
     ).astype(jnp.bfloat16)
 
     last = []
-    for offset in range(1, owners):
-        copy = pltpu.make_async_remote_copy(
-            src_ref=weights.at[me],
-            dst_ref=weights.at[me],
-            send_sem=last_send.at[offset],
-            recv_sem=last_recv.at[offset],
-            device_id=device(lax.rem(me + offset, owners)),
-            device_id_type=mesh_id,
-        )
-        copy.start()
-        last.append(copy)
+    for rank in range(chan_count):
+        for shift in range(sub_count):
+            if rank == top and shift == 0:
+                continue
+            number = rank * sub_count + shift
+            copy = pltpu.make_async_remote_copy(
+                src_ref=weights.at[me],
+                dst_ref=weights.at[me],
+                send_sem=last_send.at[number],
+                recv_sem=last_recv.at[number],
+                device_id={"chan": partners[rank], "sub": lax.rem(sub + shift, sub_count)},
+                device_id_type=mesh_id,
+            )
+            copy.start()
+            last.append(copy)
 
     def store(first, part, value):
         for number in range(half):
@@ -547,10 +583,11 @@
         store(half + degree, part, duals[part] + rho * (solved[part] - fit))
     for copy in gathers:
         copy.wait_send()
-    for copy in near.values():
-        copy.wait_send()
-    for _, copy in far:
-        copy.wait_send()
+    for rank in range(chan_count):
+        for shift in range(1, sub_count):
+            near_copy(rank, shift).wait_send()
+        if rank < top:
+            far_copy(rank).wait_send()
     for copy in last:
         copy.wait_send()
 
@@ -586,7 +623,7 @@
     bases = pairs.shape[0]
     degree = consensus.shape[0]
     width = LANES // half
-    if width & (width - 1) or stations >= width or tile_rows != LANES or directions != 8:
+    if chan_count & (chan_count - 1) or width & (width - 1) or stations >= width or tile_rows != LANES or directions != 8:
         raise ValueError("unsupported sizes")
     groups = -(-(tiles + owners * (GROUP - 1)) // GROUP)
     groups = -(-groups // UNROLL) * UNROLL
@@ -612,7 +649,7 @@
     f32, bf16, i32 = jnp.float32, jnp.bfloat16, jnp.int32
     result = pl.pallas_call(
         functools.partial(whole_kernel, chan_count, sub_count, half, groups),
-        out_shape=jax.ShapeDtypeStruct((2 * half + degree, 2, directions, LANES), f32),
+        out_shape=pltpu.VMEM((2 * half + degree, 2, directions, LANES), f32),
         in_specs=[pl.BlockSpec(memory_space=pltpu.SMEM)]
         + [pl.BlockSpec(memory_space=pl.ANY)] * len(operands),
         out_specs=pl.BlockSpec(memory_space=pltpu.VMEM),
@@ -622,13 +659,13 @@
             vmem((bases * half, 2 * tile_rows, LANES), bf16),
             vmem((LANES, tile_rows), f32),
             vmem((bases * half, 2, tile_rows), i32),
-            vmem(((tiles + 8) * 2 * directions, tile_rows), f32),
+            vmem((2, tiles + 1, directions, tile_rows), f32),
+            vmem((8 * 2 * directions, tile_rows), f32),
             vmem((2 * tiles + 8, tile_rows), f32),
             vmem((tiles + 8, tile_rows), i32),
             vmem((8, code_width), i32),
             pltpu.SMEM((8, code_width), i32),
             vmem((groups + 1, out_rows, LANES), f32),
-            vmem((2 * GROUP * UNROLL, 3, 2 * directions, LANES), f32),
             vmem((2, directions, LANES), f32),
             vmem((sub_count - 1, chan_count, coded, LANES), bf16),
             vmem((sub_count - 1, chan_count, coded, LANES), bf16),
@@ -657,7 +694,7 @@
         ),
         in_specs=[pl.BlockSpec(memory_space=pltpu.VMEM)],
         out_specs=tuple(pl.BlockSpec(memory_space=pltpu.VMEM) for _ in range(3)),
-    )(result)
+    )(pltpu.with_memory_space_constraint(result, pltpu.VMEM))
     return tuple(jnp.swapaxes(x, 2, 3) for x in outputs)
 
 

time: 39.2 us -> 34.8 us (0.89)
  Pallas kernels: 38.4 us -> 34.1 us
    pallas_call x1, Pallas kernels: 36.9 us -> 33.4 us  [body(): pl.pallas_call(functools.partial(whole_kernel, chan_count, sub_count, hal...]
    pallas_call x1, Pallas kernels: 1.47 us -> 0.63 us  [body(): pl.pallas_call(deliver_kernel, out_shape=tuple((jax.ShapeDtypeStruct(x.sh...]
where the time goes in v3:
time: 34.8 us; the launch traced here: 34.7 us
  Pallas kernels  34.1 us (98%)
  between operations  0.64 us (2%)
    pallas_call x1, Pallas kernels, body(): pl.pallas_call(functools.partial(whole_kernel, chan_count, sub_count, hal...  33.4 us

profile of v3, /device:TPU:0, one launch (start us, length us, event | category | flops | bytes accessed | tf_op | source)
XLA Modules:
  0.0 34.7 jit_solution(10606886642660299)
XLA Ops:
  0.6 33.4 %shard_map.130.result_ref = f32[8,2,8,128]{3,2,1,0:T(8,128)S(1)} custom-call(f32[8]{0:T(128)} %rho_ref.1, s32[1,512]{1,0:T(1,128)} %bitcast.16, s32[1,512]{1,0:T(1,128)} %bitcast.17, s32[1,512]{1,0:T(1,128)} %bitcast.18, bf16[8192,128]{1,0:T(8,128)(2,1)} %bitcast.11, bf16[1024,128]{1,0:T(8,128)(2,1)} %bitcast.12, s32[512,128]{1,0:T(8,128)} %keep_hbm.1, ...), custom_call_target="tpu_custom_call" | custom-call | tf_op jit(solution)/shard_map/pallas_call | solution.py:650
  34.1 0.6 %shard_map.131 = (f32[2,2,8,62]{3,2,1,0:T(8,128)}, f32[4,2,8,62]{3,2,1,0:T(8,128)}, f32[2,2,8,62]{3,2,1,0:T(8,128)}) custom-call(f32[8,2,8,128]{3,2,1,0:T(8,128)S(1)} %shard_map.130.result_ref), custom_call_target="tpu_custom_call" | custom-call | tf_op jit(solution)/shard_map/pallas_call | solution.py:690

commit v4 on v3

--- a/solution.py
+++ b/solution.py
@@ -11,6 +11,8 @@
 LANES = 128
 GROUP = 4
 UNROLL = 20
+GAIN_MOST = 5.0
+CODE_MOST = 32767.0
 
 
 def lay_pair(load, pad, half, width):
@@ -42,34 +44,34 @@
     return np.linalg.inv(basis @ basis.T)
 
 
-def end_rows(real, imag, seen_real, seen_imag, upper, sign):
+def end_rows(real, imag, seen_real, seen_imag, upper, turn, sign):
     directions = real.shape[0]
-    bf16 = jnp.bfloat16
-    flipped = -real if sign > 0 else -imag
-    def turned(number, shift):
-        return pltpu.roll((real, imag, flipped)[number], directions - shift, axis=0)
 
     def pair(first, second):
-        return jnp.concatenate([first, second], axis=0).astype(bf16)
+        return jnp.concatenate([first, second], axis=0).astype(jnp.bfloat16)
+
+    def turned(value, shift):
+        return pltpu.roll(value, directions - shift, axis=0)
 
     left, right = pair(real, real), pair(imag, imag)
-    ahead_real, ahead_imag = pair(turned(0, 1), turned(0, 2)), pair(turned(1, 1), turned(1, 2))
+    ahead_real = pair(turned(real, 1), turned(real, 2))
+    ahead_imag = pair(turned(imag, 1), turned(imag, 2))
     both = left * ahead_real + right * ahead_imag
-    cross = left * ahead_imag - right * ahead_real if sign > 0 else right * ahead_real - left * ahead_imag
+    third_real, third_imag = turned(real, 3), turned(imag, 3)
+    fourth_real, fourth_imag = turned(real, 4), turned(imag, 4)
+    ahead_one = pair(third_imag, jnp.where(upper, fourth_real, fourth_imag))
+    ahead_two = pair(third_real, jnp.where(upper, fourth_imag, fourth_real))
     if sign > 0:
-        cross_left, cross_right = (turned(1, 3), turned(1, 4)), (turned(2, 3), turned(2, 4))
-    else:
-        cross_left, cross_right = (turned(2, 3), turned(2, 4)), (turned(0, 3), turned(0, 4))
-    mixed_left = jnp.where(upper, turned(0, 4), cross_left[1])
-    mixed_right = jnp.where(upper, turned(1, 4), cross_right[1])
-    third = left * pair(turned(0, 3), mixed_left) + right * pair(turned(1, 3), mixed_right)
-    last = left * pair(cross_left[0], real) + right * pair(cross_right[0], imag)
-    side_real = real * seen_real + imag * seen_imag
-    if sign > 0:
+        cross = left * ahead_imag - right * ahead_real
+        mixed = left * ahead_one + right * turn * ahead_two
         side_imag = real * seen_imag - imag * seen_real
     else:
+        cross = right * ahead_real - left * ahead_imag
+        mixed = left * turn * ahead_one + right * ahead_two
         side_imag = imag * seen_real - real * seen_imag
-    return jnp.concatenate([both, cross, third, last, pair(side_real, side_imag)], axis=0)
+    plain = left * pair(third_real, real) + right * pair(third_imag, imag)
+    side_real = real * seen_real + imag * seen_imag
+    return jnp.concatenate([both, cross, mixed, plain, pair(side_real, side_imag)], axis=0)
 
 
 def solve_hermitian(groups_real, groups_imag, mixed, ridge, side_real, side_imag):
@@ -218,6 +220,7 @@
     duals_ref,
     consensus_ref,
     gain_table,
+    gain_codes,
     table,
     turned,
     stations_of,
@@ -301,15 +304,19 @@
     loads[0].wait()
     for owner in range(sub_count):
         for part in range(2):
-            gain_table[top * sub_count + owner, part] = lay_pair(
-                lambda number: gains_ref[owner * half + number, part], pad, half, width
+            here = lay_pair(lambda number: gains_ref[owner * half + number, part], pad, half, width)
+            gain_table[top * sub_count + owner, part] = here
+            gain_codes[top * sub_count + owner, part] = (
+                jnp.round(jnp.clip(here, -GAIN_MOST, GAIN_MOST) * (CODE_MOST / GAIN_MOST))
+                .astype(jnp.int32)
+                .astype(jnp.int16)
             )
     pl.semaphore_wait(barrier, owners - 1)
     gathers = []
     for rank in range(top):
         copy = pltpu.make_async_remote_copy(
-            src_ref=gain_table.at[pl.ds(top * sub_count, sub_count)],
-            dst_ref=gain_table.at[pl.ds(rank * sub_count, sub_count)],
+            src_ref=gain_codes.at[pl.ds(top * sub_count, sub_count)],
+            dst_ref=gain_codes.at[pl.ds(rank * sub_count, sub_count)],
             send_sem=gains_send.at[rank],
             recv_sem=gains_recv.at[rank],
             device_id={"chan": partners[rank]},
@@ -378,9 +385,13 @@
     out_rows = normal_rows + 2 * directions
     sums_ref[0] = jnp.zeros((out_rows, LANES), jnp.float32)
     upper = row < directions // 2
+    tall = lax.broadcasted_iota(jnp.int32, (2 * directions, LANES), 0)
+    turn = jnp.where((tall >= directions) & (tall < directions + directions // 2), 1.0, -1.0).astype(jnp.bfloat16)
     to_scalar.wait()
-    for copy in gathers:
+    for rank, copy in enumerate(gathers):
         copy.wait_recv()
+        span = pl.ds(rank * sub_count, sub_count)
+        gain_table[span] = gain_codes[span].astype(jnp.int32).astype(jnp.float32) * (GAIN_MOST / CODE_MOST)
 
     def spread(values):
         return jnp.broadcast_to(values, shape)
@@ -418,8 +429,8 @@
         other_real = real * near_real - imag * near_imag
         other_imag = real * near_imag + imag * near_real
         return [
-            end_rows(slope_real, slope_imag, seen_real, seen_imag, upper, 1),
-            end_rows(other_real, other_imag, seen_real, seen_imag, upper, -1),
+            end_rows(slope_real, slope_imag, seen_real, seen_imag, upper, turn, 1),
+            end_rows(other_real, other_imag, seen_real, seen_imag, upper, turn, -1),
         ], table[entry]
 
     def sums_of(rank, which):
@@ -479,13 +490,17 @@
             rows, entries = [], []
             for inner in range(GROUP):
                 ends, entry = one_tile(group * GROUP + inner)
-                rows += ends
+                rows.append(jnp.concatenate(ends, axis=1))
                 entries.append(entry)
-            total = jnp.dot(
-                jnp.concatenate(rows, axis=1),
-                jnp.concatenate(entries, axis=0),
-                preferred_element_type=jnp.float32,
-            )
+            total = None
+            for inner in range(0, GROUP, 2):
+                value = jnp.dot(
+                    jnp.concatenate(rows[inner : inner + 2], axis=0),
+                    jnp.concatenate(entries[inner : inner + 2], axis=1),
+                    preferred_element_type=jnp.float32,
+                )
+                value = value[:out_rows, :LANES] + value[out_rows:, LANES:]
+                total = value if total is None else total + value
             running = running * codes[3, group].astype(jnp.float32) + total
             sums_ref[group + 1] = running
         return carry
@@ -524,8 +539,8 @@
 
     group = [total[i * directions : (i + 1) * directions] for i in range(directions + 2)]
     solved = solve_hermitian(
-        [group[7], group[0], group[1], group[4]],
-        [group[2], group[3], group[6]],
+        [group[7], group[0], group[1], group[6]],
+        [group[2], group[3], group[4]],
         group[5],
         rho,
         group[directions] - duals[0] + rho * anchors[0],
@@ -656,6 +671,7 @@
         scratch_shapes=[vmem(x.shape, x.dtype) for x in operands]
         + [
             vmem((owners, 2, directions, LANES), f32),
+            vmem((owners, 2, directions, LANES), jnp.int16),
             vmem((bases * half, 2 * tile_rows, LANES), bf16),
             vmem((LANES, tile_rows), f32),
             vmem((bases * half, 2, tile_rows), i32),

time: 34.8 us -> 32.6 us (0.937)
  Pallas kernels: 34.1 us -> 31.8 us
    pallas_call x1, Pallas kernels: 33.4 us -> 31.1 us  [body(): pl.pallas_call(functools.partial(whole_kernel, chan_count, sub_count, hal...]
where the time goes in v4:
time: 32.6 us; the launch traced here: 32.4 us
  Pallas kernels  31.8 us (98%)
  between operations  0.64 us (2%)
    pallas_call x1, Pallas kernels, body(): pl.pallas_call(functools.partial(whole_kernel, chan_count, sub_count, hal...  31.1 us

profile of v4, /device:TPU:0, one launch (start us, length us, event | category | flops | bytes accessed | tf_op | source)
XLA Modules:
  0.0 32.4 jit_solution(10210651214815532061)
XLA Ops:
  0.6 31.1 %shard_map.130.result_ref = f32[8,2,8,128]{3,2,1,0:T(8,128)S(1)} custom-call(f32[8]{0:T(128)} %rho_ref.1, s32[1,512]{1,0:T(1,128)} %bitcast.16, s32[1,512]{1,0:T(1,128)} %bitcast.17, s32[1,512]{1,0:T(1,128)} %bitcast.18, bf16[8192,128]{1,0:T(8,128)(2,1)} %bitcast.11, bf16[1024,128]{1,0:T(8,128)(2,1)} %bitcast.12, s32[512,128]{1,0:T(8,128)} %keep_hbm.1, ...), custom_call_target="tpu_custom_call" | custom-call | tf_op jit(solution)/shard_map/pallas_call | solution.py:665
  31.8 0.6 %shard_map.131 = (f32[2,2,8,62]{3,2,1,0:T(8,128)}, f32[4,2,8,62]{3,2,1,0:T(8,128)}, f32[2,2,8,62]{3,2,1,0:T(8,128)}) custom-call(f32[8,2,8,128]{3,2,1,0:T(8,128)S(1)} %shard_map.130.result_ref), custom_call_target="tpu_custom_call" | custom-call | tf_op jit(solution)/shard_map/pallas_call | solution.py:706

commit v5 on v4

--- a/solution.py
+++ b/solution.py
@@ -9,8 +9,8 @@
 from jax.sharding import PartitionSpec as P
 
 LANES = 128
-GROUP = 4
-UNROLL = 20
+GROUP = 2
+UNROLL = 66
 GAIN_MOST = 5.0
 CODE_MOST = 32767.0
 
@@ -197,7 +197,7 @@
     sub_count,
     half,
     groups,
-    rho_ref,
+    rho_hbm,
     owner_hbm,
     channel_hbm,
     base_hbm,
@@ -209,6 +209,7 @@
     duals_hbm,
     consensus_hbm,
     out_ref,
+    rho_ref,
     owner_ref,
     channel_ref,
     base_ref,
@@ -262,9 +263,6 @@
 
     top = chan_count - 1
 
-    def device(flat):
-        return {"chan": lax.div(flat, sub_count), "sub": lax.rem(flat, sub_count)}
-
     def partner(rank):
         flips, result, bit = top - rank, chan, 1
         while bit < chan_count:
@@ -276,10 +274,15 @@
     partners = [partner(rank) for rank in range(chan_count)]
 
     barrier = pltpu.get_barrier_semaphore()
-    for offset in range(1, owners):
-        pl.semaphore_signal(
-            barrier, inc=1, device_id=device(lax.rem(me + offset, owners)), device_id_type=mesh_id
-        )
+    for rank in range(chan_count):
+        for shift in range(sub_count):
+            if rank < top or shift:
+                pl.semaphore_signal(
+                    barrier,
+                    inc=1,
+                    device_id={"chan": partners[rank], "sub": lax.rem(sub + shift, sub_count)},
+                    device_id_type=mesh_id,
+                )
 
     loads = []
     for number, (source, target) in enumerate(
@@ -294,6 +297,7 @@
             (keep_hbm, keep_ref),
             (duals_hbm, duals_ref),
             (consensus_hbm, consensus_ref),
+            (rho_hbm, rho_ref),
         ]
     ):
         copy = pltpu.make_async_copy(source, target, local_sem.at[number])
@@ -665,10 +669,10 @@
     result = pl.pallas_call(
         functools.partial(whole_kernel, chan_count, sub_count, half, groups),
         out_shape=pltpu.VMEM((2 * half + degree, 2, directions, LANES), f32),
-        in_specs=[pl.BlockSpec(memory_space=pltpu.SMEM)]
-        + [pl.BlockSpec(memory_space=pl.ANY)] * len(operands),
+        in_specs=[pl.BlockSpec(memory_space=pl.ANY)] * (len(operands) + 1),
         out_specs=pl.BlockSpec(memory_space=pltpu.VMEM),
-        scratch_shapes=[vmem(x.shape, x.dtype) for x in operands]
+        scratch_shapes=[pltpu.SMEM(rho.shape, f32)]
+        + [vmem(x.shape, x.dtype) for x in operands]
         + [
             vmem((owners, 2, directions, LANES), f32),
             vmem((owners, 2, directions, LANES), jnp.int16),
@@ -689,7 +693,7 @@
             vmem((chan_count, coded, LANES), bf16),
             vmem((owners, 2 * directions, LANES), bf16),
             vmem((degree, owners, LANES), f32),
-            dma((len(operands) + 1,)),
+            dma((len(operands) + 2,)),
             dma((chan_count,)),
             dma((chan_count,)),
             dma((sub_count - 1, chan_count)),
@@ -702,7 +706,7 @@
         compiler_params=pltpu.CompilerParams(
             collective_id=1, has_side_effects=True, vmem_limit_bytes=60 << 20
         ),
-    )(rho, *[operands[i] for i in range(len(operands))])
+    )(rho, *operands)
     outputs = pl.pallas_call(
         deliver_kernel,
         out_shape=tuple(

time: 32.6 us -> 31 us (0.951)
  Pallas kernels: 31.8 us -> 30.2 us
    pallas_call x1, Pallas kernels: 31.1 us -> 29.6 us  [body(): pl.pallas_call(functools.partial(whole_kernel, chan_count, sub_count, hal...]
where the time goes in v5:
time: 31 us; the launch traced here: 30.8 us
  Pallas kernels  30.2 us (97%)
  between operations  0.64 us (2%)
    pallas_call x1, Pallas kernels, body(): pl.pallas_call(functools.partial(whole_kernel, chan_count, sub_count, hal...  29.6 us
    pallas_call x1, Pallas kernels, body(): pl.pallas_call(deliver_kernel, out_shape=tuple((jax.ShapeDtypeStruct(x.sh...  0.63 us

profile of v5, /device:TPU:0, one launch (start us, length us, event | category | flops | bytes accessed | tf_op | source)
XLA Modules:
  0.0 30.8 jit_solution(9877390491512030926)
XLA Ops:
  0.6 29.6 %shard_map.130.result_ref = f32[8,2,8,128]{3,2,1,0:T(8,128)S(1)} custom-call(f32[8]{0:T(128)} %rho_hbm.1, s32[1,512]{1,0:T(1,128)} %bitcast.16, s32[1,512]{1,0:T(1,128)} %bitcast.17, s32[1,512]{1,0:T(1,128)} %bitcast.18, bf16[8192,128]{1,0:T(8,128)(2,1)} %bitcast.11, bf16[1024,128]{1,0:T(8,128)(2,1)} %bitcast.12, s32[512,128]{1,0:T(8,128)} %keep_hbm.1, ...), custom_call_target="tpu_custom_call" | custom-call | tf_op jit(solution)/shard_map/pallas_call | solution.py:669
  30.2 0.6 %shard_map.131 = (f32[2,2,8,62]{3,2,1,0:T(8,128)}, f32[4,2,8,62]{3,2,1,0:T(8,128)}, f32[2,2,8,62]{3,2,1,0:T(8,128)}) custom-call(f32[8,2,8,128]{3,2,1,0:T(8,128)S(1)} %shard_map.130.result_ref), custom_call_target="tpu_custom_call" | custom-call | tf_op jit(solution)/shard_map/pallas_call | solution.py:710

commit v6 on v5

--- a/solution.py
+++ b/solution.py
@@ -483,9 +483,11 @@
             def _():
                 start_near(rank)
 
-            @pl.when(step == ready + 1)
-            def _():
-                start_far(rank)
+            if ready + 1 < steps:
+
+                @pl.when(step == ready + 1)
+                def _():
+                    start_far(rank)
 
         base_group = step * UNROLL
         running = sums_ref[base_group]
@@ -514,7 +516,7 @@
     early = []
     for rank in range(top):
         ready = -(-(rank + 1) * most // (GROUP * UNROLL))
-        if ready + 1 < steps:
+        if ready < steps:
             early.append(ready)
     lax.fori_loop(0, steps, some_groups, 0)
 
@@ -534,8 +536,9 @@
             )
         anchors.append(anchor)
 
-    for rank in range(len(early), top):
-        start_far(rank)
+    for rank in range(top):
+        if rank >= len(early) or early[rank] + 1 >= steps:
+            start_far(rank)
     total = add_near(top)
     for rank in range(top):
         far_copy(rank).wait_recv()

time: 31 us -> 30.7 us (level)
  no operation moved by 1% of the time
where the time goes in v6:
time: 30.7 us; the launch traced here: 30.6 us
  Pallas kernels  29.9 us (97%)
  between operations  0.64 us (2%)
    pallas_call x1, Pallas kernels, body(): pl.pallas_call(functools.partial(whole_kernel, chan_count, sub_count, hal...  29.3 us
    pallas_call x1, Pallas kernels, body(): pl.pallas_call(deliver_kernel, out_shape=tuple((jax.ShapeDtypeStruct(x.sh...  0.63 us

profile of v6, /device:TPU:0, one launch (start us, length us, event | category | flops | bytes accessed | tf_op | source)
XLA Modules:
  0.0 30.6 jit_solution(500138385640569729)
XLA Ops:
  0.6 29.3 %shard_map.130.result_ref = f32[8,2,8,128]{3,2,1,0:T(8,128)S(1)} custom-call(f32[8]{0:T(128)} %rho_hbm.1, s32[1,512]{1,0:T(1,128)} %bitcast.16, s32[1,512]{1,0:T(1,128)} %bitcast.17, s32[1,512]{1,0:T(1,128)} %bitcast.18, bf16[8192,128]{1,0:T(8,128)(2,1)} %bitcast.11, bf16[1024,128]{1,0:T(8,128)(2,1)} %bitcast.12, s32[512,128]{1,0:T(8,128)} %keep_hbm.1, ...), custom_call_target="tpu_custom_call" | custom-call | tf_op jit(solution)/shard_map/pallas_call | solution.py:672
  30.0 0.6 %shard_map.131 = (f32[2,2,8,62]{3,2,1,0:T(8,128)}, f32[4,2,8,62]{3,2,1,0:T(8,128)}, f32[2,2,8,62]{3,2,1,0:T(8,128)}) custom-call(f32[8,2,8,128]{3,2,1,0:T(8,128)S(1)} %shard_map.130.result_ref), custom_call_target="tpu_custom_call" | custom-call | tf_op jit(solution)/shard_map/pallas_call | solution.py:713

commit v7 on v6

--- a/solution.py
+++ b/solution.py
@@ -391,6 +391,19 @@
     upper = row < directions // 2
     tall = lax.broadcasted_iota(jnp.int32, (2 * directions, LANES), 0)
     turn = jnp.where((tall >= directions) & (tall < directions + directions // 2), 1.0, -1.0).astype(jnp.bfloat16)
+    mine = [jnp.broadcast_to(basis_buf[d, pl.ds(me, 1), :], shape) for d in range(degree)]
+    duals = [
+        lay_pair(lambda number: duals_ref[number, part], pad, half, width) for part in range(2)
+    ]
+    anchors = []
+    for part in range(2):
+        anchor = jnp.zeros(shape, jnp.float32)
+        for d in range(degree):
+            anchor = anchor + mine[d] * lay_pair(
+                lambda number: consensus_ref[d, part], pad, half, width
+            )
+        anchors.append(anchor)
+
     to_scalar.wait()
     for rank, copy in enumerate(gathers):
         copy.wait_recv()
@@ -522,19 +535,6 @@
 
     for rank in range(len(early), chan_count):
         start_near(rank)
-
-    mine = [jnp.broadcast_to(basis_buf[d, pl.ds(me, 1), :], shape) for d in range(degree)]
-    duals = [
-        lay_pair(lambda number: duals_ref[number, part], pad, half, width) for part in range(2)
-    ]
-    anchors = []
-    for part in range(2):
-        anchor = jnp.zeros(shape, jnp.float32)
-        for d in range(degree):
-            anchor = anchor + mine[d] * lay_pair(
-                lambda number: consensus_ref[d, part], pad, half, width
-            )
-        anchors.append(anchor)
 
     for rank in range(top):
         if rank >= len(early) or early[rank] + 1 >= steps:

time: 30.7 us -> 30.5 us (level)
  no operation moved by 1% of the time
where the time goes in v7:
time: 30.5 us; the launch traced here: 30.4 us
  Pallas kernels  29.7 us (97%)
  between operations  0.64 us (2%)
    pallas_call x1, Pallas kernels, body(): pl.pallas_call(functools.partial(whole_kernel, chan_count, sub_count, hal...  29.1 us
    pallas_call x1, Pallas kernels, body(): pl.pallas_call(deliver_kernel, out_shape=tuple((jax.ShapeDtypeStruct(x.sh...  0.63 us

profile of v7, /device:TPU:0, one launch (start us, length us, event | category | flops | bytes accessed | tf_op | source)
XLA Modules:
  0.0 30.4 jit_solution(4022816110843627692)
XLA Ops:
  0.6 29.1 %shard_map.130.result_ref = f32[8,2,8,128]{3,2,1,0:T(8,128)S(1)} custom-call(f32[8]{0:T(128)} %rho_hbm.1, s32[1,512]{1,0:T(1,128)} %bitcast.16, s32[1,512]{1,0:T(1,128)} %bitcast.17, s32[1,512]{1,0:T(1,128)} %bitcast.18, bf16[8192,128]{1,0:T(8,128)(2,1)} %bitcast.11, bf16[1024,128]{1,0:T(8,128)(2,1)} %bitcast.12, s32[512,128]{1,0:T(8,128)} %keep_hbm.1, ...), custom_call_target="tpu_custom_call" | custom-call | tf_op jit(solution)/shard_map/pallas_call | solution.py:672
  29.7 0.6 %shard_map.131 = (f32[2,2,8,62]{3,2,1,0:T(8,128)}, f32[4,2,8,62]{3,2,1,0:T(8,128)}, f32[2,2,8,62]{3,2,1,0:T(8,128)}) custom-call(f32[8,2,8,128]{3,2,1,0:T(8,128)S(1)} %shard_map.130.result_ref), custom_call_target="tpu_custom_call" | custom-call | tf_op jit(solution)/shard_map/pallas_call | solution.py:713
